TPU v7x, 32 devices: a whole 2x2x4 slice. The times are simulated.
32 devices in a mesh: parts: 2 (over y), view: 4 (over x, core), tile: 4 (over z).
Axes of the slice: x: 2, y: 2, z: 4, core: 2. Of those that a mesh axis runs over, the one named last changes fastest.
Arguments:
- data: float32 [8, 32, 48, 32], P(('parts', 'view'), 'tile'), parts along dimension 0, may hold values from 0.25 to 4
- labels: int32 [8, 32, 48, 32], P(('parts', 'view'), 'tile'), parts along dimension 0, may hold values from 0 to 3
- kernel: float32 [4, 32, 9], P('view'), may hold values from 0.1 to 1
- offsets: int32 [4, 32], P('view'), may hold values from -2 to 2
Outputs:
- estimate: float32 [8, 32, 48, 32], P(('parts', 'view'), 'tile'), parts along dimension 0
There are 2 independent parts, one for each index of `parts`. A program takes and returns all parts, laid end to end along the dimension named above; an argument that names none is the same for every part. Nothing has to cross between parts.
All inputs are finite; a program needn't handle non-finite values.
Results may differ from a plain program's by a relative error of at most 0.000088.
Values sent between devices are 32-bit elements; how exact they have to be, the bound alone decides.
A program may use at most 64 MiB of HBM per device.

v0:
```python
import functools

import jax
import jax.numpy as jnp
from jax import lax
from jax.experimental import pallas as pl
from jax.experimental.pallas import tpu as pltpu
from jax.sharding import PartitionSpec as P

ITERS = 2
SWEEPS = 4


WEAK = 0.2
TAU = 0.15


def extended(cells, sides, width):
    for axis, dim in sides:
        count = lax.axis_size(axis)
        ends = count - 1
        head = lax.slice_in_dim(cells, 0, width, axis=dim)
        tail = lax.slice_in_dim(cells, cells.shape[dim] - width, cells.shape[dim], axis=dim)
        cells = jnp.concatenate(
            [
                lax.ppermute(tail, axis, [(i, (i + 1) % count) for i in range(ends)]),
                cells,
                lax.ppermute(head, axis, [((i + 1) % count, i) for i in range(ends)]),
            ],
            axis=dim,
        )
    return cells


def swapped(block, axis, stride):
    count = lax.axis_size(axis)
    route = []
    for low in range(count):
        high = low | 1 << stride
        if high != low and high < count:
            route += [(low, high), (high, low)]
    return lax.ppermute(block, axis, route)


def band(kernel, offsets):
    depth_cells = kernel.shape[0]
    taps = jnp.arange(kernel.shape[1], dtype=jnp.int32) - 4
    depth = jnp.arange(depth_cells, dtype=jnp.int32)
    index = jnp.clip(depth[:, None] + taps[None, :] + offsets[:, None], 0, depth_cells - 1)
    weight = kernel / jnp.sum(kernel, axis=1, keepdims=True)
    return (index, weight)


def axis_term(field, region, axis):
    count = field.shape[axis]
    upper = lax.slice_in_dim(field, 1, count, axis=axis)
    lower = lax.slice_in_dim(field, 0, count - 1, axis=axis)
    same = jnp.where(
        lax.slice_in_dim(region, 1, count, axis=axis)
        == lax.slice_in_dim(region, 0, count - 1, axis=axis),
        1.0,
        WEAK,
    )
    flux = same * (upper - lower)
    after = [(0, 0)] * 3
    before = [(0, 0)] * 3
    after[axis] = (0, 1)
    before[axis] = (1, 0)
    return jnp.pad(flux, after) - jnp.pad(flux, before)


def sweep_rows(field, region, first_row, total_rows):
    extent = field.shape[0]
    global_rows = first_row + jnp.arange(extent, dtype=jnp.int32)
    inside = ((global_rows >= 0) & (global_rows < total_rows)).astype(field.dtype)[:, None, None]
    same = jnp.where(region[1:] == region[:-1], 1.0, WEAK) * inside[1:] * inside[:-1]
    flux = same * (field[1:] - field[:-1])
    inner = field[1:-1]
    inner_labels = region[1:-1]
    total = (
        flux[1:] - flux[:-1] + axis_term(inner, inner_labels, 1) + axis_term(inner, inner_labels, 2)
    )
    return inner + TAU * total


def regroup(received, tiles):
    slab, rows, depth_cells = received.shape
    blocks = received.reshape(slab, rows, tiles, depth_cells // tiles)
    return blocks.transpose(3, 1, 2, 0).reshape(depth_cells // tiles, rows, depth_cells)


def on_device(data, labels, kernel, offsets):
    recorded = data[0]
    region = labels[0]
    index, weight = band(kernel[0], offsets[0])
    tiles = lax.axis_size("tile")
    slab, rows, depth_cells = recorded.shape
    total_rows = slab * tiles
    start = lax.axis_index("tile") * slab
    parity = lax.axis_index("view") % 2
    columns = jnp.arange(depth_cells, dtype=jnp.int32)
    matrix = jnp.sum(weight[:, :, None] * (index[:, :, None] == columns[None, None, :]), axis=1)
    label_ext = extended(region, (("tile", 0),), 4)
    current = recorded
    for step in range(ITERS):
        forward_flat = jnp.dot(
            current.reshape(-1, depth_cells), matrix.T, precision=lax.Precision.HIGHEST
        )
        field = recorded / forward_flat.reshape(current.shape)
        flat = jnp.dot(field.reshape(-1, depth_cells), matrix, precision=lax.Precision.HIGHEST)
        correction = flat.reshape(field.shape)
        turned = correction
        for repeat in range(2):
            turned = regroup(
                lax.all_to_all(
                    jnp.flip(turned, 2), "tile", split_axis=2, concat_axis=2, tiled=True
                ),
                tiles,
            )
        turned = swapped(turned, "view", 1)
        paired = jnp.sqrt(correction * turned)
        outgoing = jnp.where(parity == 0, jnp.flip(paired, 2), paired)
        rotated = regroup(
            lax.all_to_all(outgoing, "tile", split_axis=2, concat_axis=2, tiled=True), tiles
        )
        rotated = jnp.where(parity == 1, jnp.flip(rotated, 2), rotated)
        partner = swapped(rotated, "view", 0)
        current = current * jnp.sqrt(paired * partner)
        widened = extended(current, (("tile", 0),), 4)
        for sweep in range(SWEEPS):
            extent = widened.shape[0]
            widened = sweep_rows(
                widened, label_ext[sweep : sweep + extent], start - 4 + sweep, total_rows
            )
        current = widened
    return current[None]


def gathered(parts, b_of, slot, depth):
    fold = len(parts)
    lanes = parts[0].shape[1]
    total = None
    for k in range(fold):
        amount = (depth * (k - b_of[k])) % lanes
        piece = pltpu.roll(parts[k], amount, 1) if amount else parts[k]
        total = piece if total is None else jnp.where(slot == k, piece, total)
    return total


def turning(lanes, depth, flip_z):
    row_ids = lax.broadcasted_iota(jnp.int32, (lanes, lanes), 0)
    lane_ids = lax.broadcasted_iota(jnp.int32, (lanes, lanes), 1)
    same_block = (row_ids // depth) == (lane_ids // depth)
    aim = jnp.where(flip_z, depth - 1 - lane_ids % depth, lane_ids % depth)
    return same_block, jnp.where(same_block & (row_ids % depth == aim), 1.0, 0.0).astype(jnp.float32)


def exact(a, b):
    return jnp.dot(a, b, precision=lax.Precision.HIGHEST, preferred_element_type=jnp.float32)


def product(a, b, contract):
    return lax.dot_general(a, b, (contract, ((), ())), preferred_element_type=jnp.float32)


def halves(a):
    high = a.astype(jnp.bfloat16)
    return high, (a - high.astype(jnp.float32)).astype(jnp.bfloat16)


def permuted(a, turn):
    high, low = halves(a)
    turn = turn.astype(jnp.bfloat16)
    return product(high, turn, ((1,), (0,))) + product(low, turn, ((1,), (0,)))


def blurred(a, matrix, contract):
    high, low = halves(a)
    return product(high, matrix[0], contract) + (
        product(low, matrix[0], contract) + product(high, matrix[1], contract)
    )


def laid_out(back_ref, out_ref, back, mixed, unpacked, in_sem, out_sem):
    copy = pltpu.make_async_copy(back_ref, back, in_sem)
    copy.start()
    slab, depth, rows = out_ref.shape[1:]
    groups, _, lanes = back.shape
    fold = lanes // depth
    blocks = mixed.shape[0]
    view = lax.axis_index("view")
    flip_x = (view == 1) | (view == 2)
    _, turn = turning(lanes, depth, view >= 2)
    slot = lax.broadcasted_iota(jnp.int32, (mixed.shape[1] // fold, lanes), 1) // depth
    copy.wait()
    results = []
    for j in range(blocks):
        parts = []
        for k in range(fold):
            line = back[:, fold * j + k, :]
            parts.append(
                jnp.concatenate(
                    [line, jnp.zeros((mixed.shape[1] // fold - groups, lanes), jnp.float32)], axis=0
                )
            )
        for b in range(fold):
            mixed[j, pl.ds(b, mixed.shape[1] // fold, stride=fold), :] = gathered(
                parts, [b] * fold, slot, depth
            )
        unpacked[lanes * j : lanes * (j + 1), :] = permuted(mixed[j, 0:rows], turn).T
        for k in range(fold):
            x = fold * j + k
            copy = pltpu.make_async_copy(
                unpacked.at[pl.ds(x * depth, depth)],
                out_ref.at[0, jnp.where(flip_x, slab - 1 - x, x)],
                out_sem.at[x],
            )
            copy.start()
            results.append(copy)
    for copy in results:
        copy.wait()


def fused(tiles, data_ref, labels_ref, taps_ref, shift_ref, back, raw, raw_labels, taps_buf, shift_buf, mixed, packed, packed_labels, held, held_labels, mats, est, coef, outgoing, incoming, halo, in_sem, send, recv, send_l, recv_l, send_m, recv_m, send_p, recv_p, send_h, recv_h, send_o, recv_o):
    mesh_id = pl.DeviceIdType.MESH
    slab, depth, rows = data_ref.shape[1:]
    lanes = packed.shape[2]
    fold = lanes // depth
    groups = rows // fold
    per_tile = groups // tiles
    width = held.shape[1]
    cells = held.shape[2]
    peers = 2 * tiles
    view = lax.axis_index("view")
    tile = lax.axis_index("tile")
    part = lax.axis_index("parts")
    half = view // 2
    core = view % 2
    me = half * tiles + tile
    role = (half + tile) % 2
    flip_x = (view == 1) | (view == 2)
    flip_z = view >= 2

    def peer(q):
        return (part, 2 * (q // tiles) + core, q % tiles)

    copies_in = []
    for source, target, base in ((data_ref, raw, 0), (labels_ref, raw_labels, slab)):
        for x in range(slab):
            at = jnp.where(flip_x, slab - 1 - x, x)
            copies_in.append(
                pltpu.make_async_copy(
                    source.at[0, x],
                    target.at[pl.ds(pl.multiple_of(at * depth, 8), depth)],
                    in_sem.at[base + x],
                )
            )
    copies_in.append(pltpu.make_async_copy(taps_ref, taps_buf, in_sem.at[2 * slab]))
    copies_in.append(pltpu.make_async_copy(shift_ref, shift_buf, in_sem.at[2 * slab + 1]))
    for copy in copies_in:
        copy.start()

    barrier = pltpu.get_barrier_semaphore()
    across = (part, 2 * half + 1 - core, tile)
    for d in range(1, peers):
        pl.semaphore_signal(barrier, inc=1, device_id=peer((me + d) % peers), device_id_type=mesh_id)
    pl.semaphore_signal(barrier, inc=1, device_id=across, device_id_type=mesh_id)

    same_block, turn = turning(lanes, depth, flip_z)
    slot = lax.broadcasted_iota(jnp.int32, (mixed.shape[1] // fold, lanes), 1) // depth
    blocks = slab * depth // lanes

    def pack(source, target, fill, turner):
        edge = jnp.full((1, slab, lanes), fill, jnp.float32)
        target[0:1] = edge
        target[groups + 1 : groups + 2] = edge
        for j in range(blocks):
            mixed[j, 0:rows] = turner(source[lanes * j : lanes * (j + 1), :])
        for j in range(blocks):
            parts = [
                mixed[j, pl.ds(b, mixed.shape[1] // fold, stride=fold), :] for b in range(fold)
            ]
            for k in range(fold):
                line = gathered(parts, [k] * fold, slot, depth)
                target[1 : groups + 1, fold * j + k, :] = line[:groups]

    def turned_labels(block):
        block = block.astype(jnp.float32).T.astype(jnp.bfloat16)
        return product(block, turn.astype(jnp.bfloat16), ((1,), (0,)))

    spot = pl.ds(pl.multiple_of(jnp.where(flip_x, tiles - 1 - tile, tile) * slab, 8), slab)

    def scatter(source, target, send_sem, recv_sem):
        copies = []
        for d in range(peers):
            q = (me + d) % peers
            src = source.at[pl.ds(per_tile * (q % tiles) + (q // tiles + q % tiles) % 2, width)]
            dst = target.at[half, :, spot, :]
            if d == 0:
                copy = pltpu.make_async_copy(src, dst, recv_sem.at[0])
            else:
                copy = pltpu.make_async_remote_copy(
                    src_ref=src,
                    dst_ref=dst,
                    send_sem=send_sem.at[d],
                    recv_sem=recv_sem.at[d],
                    device_id=peer(q),
                    device_id_type=mesh_id,
                )
            copy.start()
            copies.append(copy)
        return copies

    def landed(copies):
        copies[0].wait()
        for copy in copies[1:]:
            copy.wait_recv()

    for x in range(slab):
        copies_in[x].wait()
    pack(raw, packed, 1.0, lambda v: permuted(v.T, turn))
    pl.semaphore_wait(barrier, peers)
    data_copies = scatter(packed, held, send, recv)

    copies_in[2 * slab].wait()
    copies_in[2 * slab + 1].wait()
    count = taps_buf.shape[0]
    taps = [jnp.concatenate([taps_buf[k]] * fold, axis=1) for k in range(count)]
    scale = taps[0]
    for k in range(1, count):
        scale = scale + taps[k]
    shift = jnp.concatenate([shift_buf[...]] * fold, axis=1)
    level = lax.broadcasted_iota(jnp.int32, (1, lanes), 1) % depth
    strip_row = lax.broadcasted_iota(jnp.int32, (depth, lanes), 0)
    strip_aim = jnp.where(flip_z, depth - 1 - strip_row, strip_row)
    strip = jnp.zeros((depth, lanes), jnp.float32)
    for k in range(count):
        index = jnp.clip(level + (k - 4) + shift, 0, depth - 1)
        strip = strip + jnp.where(index == strip_aim, taps[k] / scale, 0.0)
    strip = exact(strip, turn)
    mats[pl.ds(half, 1)] = strip[None]
    mat_copy = pltpu.make_async_remote_copy(
        src_ref=mats.at[half],
        dst_ref=mats.at[half],
        send_sem=send_m,
        recv_sem=recv_m,
        device_id=(part, 2 * (1 - half) + core, tile),
        device_id_type=mesh_id,
    )
    mat_copy.start()

    for x in range(slab):
        copies_in[slab + x].wait()
    pack(raw_labels, packed_labels, 0.0, turned_labels)
    label_copies = scatter(packed_labels, held_labels, send_l, recv_l)

    lane = lax.broadcasted_iota(jnp.int32, (cells, lanes), 1)
    sub = lax.broadcasted_iota(jnp.int32, (cells, lanes), 0)
    first = per_tile * tile - 1 + role
    last_lane = lane < lanes - depth
    first_lane = lane < depth

    def ahead_y(fields, g):
        return jnp.where(
            last_lane,
            pltpu.roll(fields[g], lanes - depth, 1),
            pltpu.roll(fields[(g + 1) % width], lanes - depth, 1),
        )

    def behind_y(fields, g):
        return jnp.where(
            first_lane,
            pltpu.roll(fields[g - 1], depth, 1),
            pltpu.roll(fields[g], depth, 1),
        )

    def transposed(p, chosen):
        flipped = p.T
        result = []
        for g in chosen:
            piece = flipped[0:depth]
            if g:
                piece = pltpu.roll(piece, (lanes - depth * g) % lanes, 1)
            for b in range(1, fold):
                part_b = flipped[depth * b : depth * (b + 1)]
                amount = (depth * (b - g)) % lanes
                if amount:
                    part_b = pltpu.roll(part_b, amount, 1)
                piece = jnp.where(lane // depth == b, part_b, piece)
            result.append(piece)
        return result

    landed(data_copies)
    mat_copy.wait_recv()
    blurs = [
        halves(jnp.where(same_block, jnp.concatenate([mats[s]] * fold, axis=0), 0.0))
        for s in range(2)
    ]

    def paired_of(step, chosen):
        corrections = []
        for s in range(2):
            recorded = jnp.concatenate([held[s, g] for g in chosen], axis=0)
            if step == 0:
                current = recorded
            else:
                current = jnp.concatenate([est[s, g] for g in chosen], axis=0)
            ratio = recorded / blurred(current, blurs[s], ((1,), (0,)))
            corrections.append(blurred(ratio, blurs[s], ((1,), (1,))))
        return jnp.sqrt(corrections[0] * corrections[1])

    def swapped_over(step, number, begin, size):
        copy = pltpu.make_async_remote_copy(
            src_ref=outgoing.at[step, pl.ds(begin, size)],
            dst_ref=incoming.at[step, pl.ds(begin, size)],
            send_sem=send_p.at[step, number],
            recv_sem=recv_p.at[step, number],
            device_id=across,
            device_id_type=mesh_id,
        )
        copy.start()
        pending.append(copy)
        return copy

    far = tile + 2 * role - 1
    exists = (far >= 0) & (far < tiles)

    def leaving(s, d, middle, relation):
        t = (tile + d) % tiles
        place = jnp.where(core == 1 - s, tiles - 1 - t, t)
        here = 2 - role if middle else 1 + role
        there = per_tile * tile + (1 if middle else 2 * role)
        src = est.at[s, here, pl.ds(pl.multiple_of(place * slab, 8), slab), :]
        if relation is None:
            return pltpu.make_async_copy(src, back.at[there], recv_o.at[0, middle])
        return pltpu.make_async_remote_copy(
            src_ref=src,
            dst_ref=back.at[there],
            send_sem=send_o.at[s, 2 * d + middle],
            recv_sem=recv_o.at[relation, 2 * d + middle],
            device_id=(part, 2 * s + core, t),
            device_id_type=mesh_id,
        )

    def arrived(d, middle, relation):
        origin = (tile + tiles - d) % tiles
        its_role = (half + relation + origin) % 2
        there = per_tile * origin + (1 if middle else 2 * its_role)
        pltpu.make_async_remote_copy(
            src_ref=back.at[there],
            dst_ref=back.at[there],
            send_sem=send_o.at[0, 2 * d + middle],
            recv_sem=recv_o.at[relation, 2 * d + middle],
            device_id=across,
            device_id_type=mesh_id,
        ).wait_recv()

    def send_back(s):
        for d in range(1, tiles):
            leaving(s, d, 0, (s + half) % 2).start()

        @pl.when(half == 1 - s)
        def _():
            leaving(s, 0, 0, 1).start()

        @pl.when(half == s)
        def _():
            for d in range(1, tiles):
                leaving(s, d, 1, 0).start()
            for middle in range(2):
                leaving(s, 0, middle, None).start()

    def sent_back(s):
        for d in range(1, tiles):
            leaving(s, d, 0, (s + half) % 2).wait_send()

        @pl.when(half == 1 - s)
        def _():
            leaving(s, 0, 0, 1).wait_send()

        @pl.when(half == s)
        def _():
            for d in range(1, tiles):
                leaving(s, d, 1, 0).wait_send()
            for middle in range(2):
                leaving(s, 0, middle, None).wait()

    pending = []
    ready = {}
    for step in range(ITERS):
        if step == 0:
            whole = paired_of(0, range(width))
            for g, piece in enumerate(transposed(whole, range(width))):
                outgoing[step, g] = piece
                ready[g] = whole[cells * g : cells * (g + 1)]
            swaps = [swapped_over(step, 0, 0, width)]
        else:
            inner = range(1, width - 1)
            outer = (0, width - 1)
            swaps = []
            for number, chosen in enumerate((inner, outer)):
                if number:
                    near = (width - 1) * (1 - role)
                    for s in range(2):
                        near_copies[s].wait()
                        est[s, pl.ds(near, 1)] = halo[step - 1, 1 - role, s][None]

                    @pl.when(exists)
                    def _():
                        for s in range(2):
                            far_copies[s].wait()
                            est[s, pl.ds((width - 1) * role, 1)] = halo[step - 1, role, s][None]

                part_p = paired_of(step, chosen)
                turned_p = transposed(jnp.concatenate([part_p, part_p], axis=0), range(len(chosen)))
                for k, g in enumerate(chosen):
                    outgoing[step, g] = turned_p[k]
                    ready[g] = part_p[cells * k : cells * (k + 1)]
                if number:
                    swaps += [swapped_over(step, 1 + k, g, 1) for k, g in enumerate(chosen)]
                else:
                    swaps.append(swapped_over(step, 0, 1, width - 2))
        if step == 0:
            landed(label_copies)
            for s in range(2):
                regions = [held_labels[s, g] for g in range(width)]
                for g in range(width):
                    mine = regions[g]
                    strong, weak = TAU, TAU * WEAK
                    e_x = jnp.where(pltpu.roll(mine, cells - 1, 0) == mine, strong, weak)
                    coef[0, s, g] = jnp.where(sub == cells - 1, 0.0, e_x)
                    e_z = jnp.where(pltpu.roll(mine, lanes - 1, 1) == mine, strong, weak)
                    coef[1, s, g] = jnp.where(lane % depth == depth - 1, 0.0, e_z)
                    e_y = jnp.where(ahead_y(regions, g) == mine, strong, weak)
                    y = fold * (first + g) + lane // depth
                    coef[2, s, g] = jnp.where((y >= 0) & (y < rows - 1), e_y, 0.0)
        for swap in swaps:
            swap.wait_recv()
        joined = [jnp.sqrt(ready[g] * incoming[step, g]) for g in range(width)]
        last = step == ITERS - 1
        near_copies, far_copies = [], []
        for s in range(2):
            base = held if step == 0 else est
            fields = [base[s, g] * joined[g] for g in range(width)]
            for sweep in range(SWEEPS):
                kept = range(1, width - 1) if sweep == SWEEPS - 1 else range(width)
                flux_y = {
                    g: coef[2, s, g] * (ahead_y(fields, g) - fields[g])
                    for g in range(kept[0] - 1 if kept[0] else 0, kept[-1] + 1)
                }
                if kept[0] == 0:
                    flux_y[-1] = flux_y[width - 1]
                fresh = list(fields)
                for g in kept:
                    f = fields[g]
                    flux_x = coef[0, s, g] * (pltpu.roll(f, cells - 1, 0) - f)
                    flux_z = coef[1, s, g] * (pltpu.roll(f, lanes - 1, 1) - f)
                    total = (
                        (flux_x - pltpu.roll(flux_x, 1, 0))
                        + (flux_y[g] - behind_y(flux_y, g))
                        + (flux_z - pltpu.roll(flux_z, 1, 1))
                    )
                    fresh[g] = f + total
                fields = fresh
            for g in range(width):
                est[s, g] = fields[g]
            if last:
                send_back(s)
                continue

            def shifted(number, side, x_of, target):
                return pltpu.make_async_remote_copy(
                    src_ref=est.at[s, 1 + role],
                    dst_ref=halo.at[step, side, s],
                    send_sem=send_h.at[step, number, s],
                    recv_sem=recv_h.at[step, number, s],
                    device_id=(part, 2 * x_of + core, target),
                    device_id_type=mesh_id,
                )

            near_copies.append(shifted(0, role, 1 - half, tile))
            far_copies.append(shifted(1, 1 - role, half, jnp.clip(far, 0, tiles - 1)))
            near_copies[s].start()

            @pl.when(exists)
            def _():
                far_copies[s].start()

    for d in range(tiles):
        arrived(d, 0, 1)
        if d:
            arrived(d, 0, 0)
            arrived(d, 1, 0)
    for s in range(2):
        sent_back(s)
    for copy in data_copies[1:] + label_copies[1:] + [mat_copy] + pending:
        copy.wait_send()


def by_rows(data, labels, kernel, offsets):
    tiles = lax.axis_size("tile")
    _, slab, rows, depth = data.shape
    fold = 128 // depth
    tall = -(-rows // (8 * fold)) * 8 * fold
    groups = rows // fold
    cells = slab * tiles
    peers = 2 * tiles
    width = 4
    flat = (slab * depth, rows)
    wide = (2, width, cells, 128)
    dma = pltpu.SemaphoreType.DMA
    taps = kernel.transpose(2, 0, 1)
    back = pl.pallas_call(
        functools.partial(fused, tiles),
        out_shape=jax.ShapeDtypeStruct((groups, slab, 128), jnp.float32),
        in_specs=[pl.BlockSpec(memory_space=pltpu.HBM)] * 4,
        out_specs=pl.BlockSpec(memory_space=pl.ANY),
        scratch_shapes=[
            pltpu.VMEM(flat, jnp.float32),
            pltpu.VMEM(flat, jnp.int32),
            pltpu.VMEM(taps.shape, jnp.float32),
            pltpu.VMEM(offsets.shape, jnp.int32),
            pltpu.VMEM((slab * depth // 128, tall, 128), jnp.float32),
            pltpu.VMEM((groups + 2, slab, 128), jnp.float32),
            pltpu.VMEM((groups + 2, slab, 128), jnp.float32),
            pltpu.VMEM(wide, jnp.float32),
            pltpu.VMEM(wide, jnp.float32),
            pltpu.VMEM((2, depth, 128), jnp.float32),
            pltpu.VMEM(wide, jnp.float32),
            pltpu.VMEM((3,) + wide, jnp.float32),
            pltpu.VMEM((ITERS,) + wide[1:], jnp.float32),
            pltpu.VMEM((ITERS,) + wide[1:], jnp.float32),
            pltpu.VMEM((ITERS - 1, 2, 2, cells, 128), jnp.float32),
            dma((2 * slab + 2,)),
            dma((peers,)),
            dma((peers,)),
            dma((peers,)),
            dma((peers,)),
            dma(()),
            dma(()),
            dma((ITERS, 3)),
            dma((ITERS, 3)),
            dma((ITERS - 1, 2, 2)),
            dma((ITERS - 1, 2, 2)),
            dma((2, peers)),
            dma((2, peers)),
        ],
        compiler_params=pltpu.CompilerParams(
            collective_id=0, has_side_effects=True
        ),
    )(data.transpose(0, 1, 3, 2), labels.transpose(0, 1, 3, 2), taps, offsets)
    result = pl.pallas_call(
        laid_out,
        out_shape=jax.ShapeDtypeStruct((1, slab, depth, rows), jnp.float32),
        in_specs=[pl.BlockSpec(memory_space=pl.ANY)],
        out_specs=pl.BlockSpec(memory_space=pltpu.HBM),
        scratch_shapes=[
            pltpu.VMEM((groups, slab, 128), jnp.float32),
            pltpu.VMEM((slab * depth // 128, tall, 128), jnp.float32),
            pltpu.VMEM(flat, jnp.float32),
            dma(()),
            dma((slab,)),
        ],
    )(back)
    return result.transpose(0, 1, 3, 2)


def fits(data, tiles, views):
    _, slab, rows, depth = data.shape
    return (
        views == 4
        and depth * 4 == 128
        and slab * tiles == depth
        and slab % 8 == 0
        and rows == 12 * tiles
    )


def program(data, labels, kernel, offsets):
    if fits(data, lax.axis_size("tile"), lax.axis_size("view")):
        return by_rows(data, labels, kernel, offsets)
    return on_device(data, labels, kernel, offsets)


def solution(mesh):
    placed = (
        P(("parts", "view"), "tile", None, None),
        P(("parts", "view"), "tile", None, None),
        P("view", None, None),
        P("view", None),
    )
    return jax.shard_map(
        program,
        mesh=mesh,
        in_specs=placed,
        out_specs=P(("parts", "view"), "tile", None, None),
        check_vma=False,
    )
```

profile of v0, /device:TPU:0, one launch (start us, length us, event | category | flops | bytes accessed | tf_op | source)
XLA Modules:
  0.0 26.2 jit_solution(16596437355705645191)
XLA Ops:
  0.0 24.4 %shard_map.46.back_ref = f32[12,8,128]{2,1,0:T(8,128)} custom-call(f32[1,8,32,48]{3,2,1,0:T(8,128)} %bitcast.4, s32[1,8,32,48]{3,2,1,0:T(8,128)} %bitcast.5, f32[9,1,32]{2,1,0:T(1,128)} %bitcast.6, s32[1,32]{1,0:T(1,128)} %shift_ref.1), custom_call_target="tpu_custom_call" | custom-call | tf_op jit(solution)/shard_map/pallas_call | solution.py:613
  24.4 1.9 %shard_map.47 = f32[1,8,32,48]{3,2,1,0:T(8,128)} custom-call(f32[12,8,128]{2,1,0:T(8,128)} %shard_map.46.back_ref), custom_call_target="tpu_custom_call" | custom-call | tf_op jit(solution)/shard_map/pallas_call | solution.py:652
where the time goes:
time: 26.5 us; the launch traced here: 26.2 us
  Pallas kernels  26.2 us (99%)
    pallas_call x1, Pallas kernels, by_rows(): pl.pallas_call(functools.partial(fused, tiles), out_shape=jax.ShapeDtypeS...  24.4 us
    pallas_call x1, Pallas kernels, by_rows(): pl.pallas_call(laid_out, out_shape=jax.ShapeDtypeStruct((1, slab, depth,...  1.86 us

commit v1 on v0

v1 whole, which is shorter than its diff:
```python
import functools

import jax
import jax.numpy as jnp
from jax import lax
from jax.experimental import pallas as pl
from jax.experimental.pallas import tpu as pltpu
from jax.sharding import PartitionSpec as P

ITERS = 2
SWEEPS = 4


WEAK = 0.2
TAU = 0.15


def extended(cells, sides, width):
    for axis, dim in sides:
        count = lax.axis_size(axis)
        ends = count - 1
        head = lax.slice_in_dim(cells, 0, width, axis=dim)
        tail = lax.slice_in_dim(cells, cells.shape[dim] - width, cells.shape[dim], axis=dim)
        cells = jnp.concatenate(
            [
                lax.ppermute(tail, axis, [(i, (i + 1) % count) for i in range(ends)]),
                cells,
                lax.ppermute(head, axis, [((i + 1) % count, i) for i in range(ends)]),
            ],
            axis=dim,
        )
    return cells


def swapped(block, axis, stride):
    count = lax.axis_size(axis)
    route = []
    for low in range(count):
        high = low | 1 << stride
        if high != low and high < count:
            route += [(low, high), (high, low)]
    return lax.ppermute(block, axis, route)


def band(kernel, offsets):
    depth_cells = kernel.shape[0]
    taps = jnp.arange(kernel.shape[1], dtype=jnp.int32) - 4
    depth = jnp.arange(depth_cells, dtype=jnp.int32)
    index = jnp.clip(depth[:, None] + taps[None, :] + offsets[:, None], 0, depth_cells - 1)
    weight = kernel / jnp.sum(kernel, axis=1, keepdims=True)
    return (index, weight)


def axis_term(field, region, axis):
    count = field.shape[axis]
    upper = lax.slice_in_dim(field, 1, count, axis=axis)
    lower = lax.slice_in_dim(field, 0, count - 1, axis=axis)
    same = jnp.where(
        lax.slice_in_dim(region, 1, count, axis=axis)
        == lax.slice_in_dim(region, 0, count - 1, axis=axis),
        1.0,
        WEAK,
    )
    flux = same * (upper - lower)
    after = [(0, 0)] * 3
    before = [(0, 0)] * 3
    after[axis] = (0, 1)
    before[axis] = (1, 0)
    return jnp.pad(flux, after) - jnp.pad(flux, before)


def sweep_rows(field, region, first_row, total_rows):
    extent = field.shape[0]
    global_rows = first_row + jnp.arange(extent, dtype=jnp.int32)
    inside = ((global_rows >= 0) & (global_rows < total_rows)).astype(field.dtype)[:, None, None]
    same = jnp.where(region[1:] == region[:-1], 1.0, WEAK) * inside[1:] * inside[:-1]
    flux = same * (field[1:] - field[:-1])
    inner = field[1:-1]
    inner_labels = region[1:-1]
    total = (
        flux[1:] - flux[:-1] + axis_term(inner, inner_labels, 1) + axis_term(inner, inner_labels, 2)
    )
    return inner + TAU * total


def regroup(received, tiles):
    slab, rows, depth_cells = received.shape
    blocks = received.reshape(slab, rows, tiles, depth_cells // tiles)
    return blocks.transpose(3, 1, 2, 0).reshape(depth_cells // tiles, rows, depth_cells)


def on_device(data, labels, kernel, offsets):
    recorded = data[0]
    region = labels[0]
    index, weight = band(kernel[0], offsets[0])
    tiles = lax.axis_size("tile")
    slab, rows, depth_cells = recorded.shape
    total_rows = slab * tiles
    start = lax.axis_index("tile") * slab
    parity = lax.axis_index("view") % 2
    columns = jnp.arange(depth_cells, dtype=jnp.int32)
    matrix = jnp.sum(weight[:, :, None] * (index[:, :, None] == columns[None, None, :]), axis=1)
    label_ext = extended(region, (("tile", 0),), 4)
    current = recorded
    for step in range(ITERS):
        forward_flat = jnp.dot(
            current.reshape(-1, depth_cells), matrix.T, precision=lax.Precision.HIGHEST
        )
        field = recorded / forward_flat.reshape(current.shape)
        flat = jnp.dot(field.reshape(-1, depth_cells), matrix, precision=lax.Precision.HIGHEST)
        correction = flat.reshape(field.shape)
        turned = correction
        for repeat in range(2):
            turned = regroup(
                lax.all_to_all(
                    jnp.flip(turned, 2), "tile", split_axis=2, concat_axis=2, tiled=True
                ),
                tiles,
            )
        turned = swapped(turned, "view", 1)
        paired = jnp.sqrt(correction * turned)
        outgoing = jnp.where(parity == 0, jnp.flip(paired, 2), paired)
        rotated = regroup(
            lax.all_to_all(outgoing, "tile", split_axis=2, concat_axis=2, tiled=True), tiles
        )
        rotated = jnp.where(parity == 1, jnp.flip(rotated, 2), rotated)
        partner = swapped(rotated, "view", 0)
        current = current * jnp.sqrt(paired * partner)
        widened = extended(current, (("tile", 0),), 4)
        for sweep in range(SWEEPS):
            extent = widened.shape[0]
            widened = sweep_rows(
                widened, label_ext[sweep : sweep + extent], start - 4 + sweep, total_rows
            )
        current = widened
    return current[None]


def gathered(parts, b_of, slot, depth):
    fold = len(parts)
    lanes = parts[0].shape[1]
    total = None
    for k in range(fold):
        amount = (depth * (k - b_of[k])) % lanes
        piece = pltpu.roll(parts[k], amount, 1) if amount else parts[k]
        total = piece if total is None else jnp.where(slot == k, piece, total)
    return total


def turning(lanes, depth, flip_z):
    row_ids = lax.broadcasted_iota(jnp.int32, (lanes, lanes), 0)
    lane_ids = lax.broadcasted_iota(jnp.int32, (lanes, lanes), 1)
    same_block = (row_ids // depth) == (lane_ids // depth)
    aim = jnp.where(flip_z, depth - 1 - lane_ids % depth, lane_ids % depth)
    return same_block, jnp.where(same_block & (row_ids % depth == aim), 1.0, 0.0).astype(jnp.float32)


def exact(a, b):
    return jnp.dot(a, b, precision=lax.Precision.HIGHEST, preferred_element_type=jnp.float32)


def product(a, b, contract):
    return lax.dot_general(a, b, (contract, ((), ())), preferred_element_type=jnp.float32)


def halves(a):
    high = a.astype(jnp.bfloat16)
    return high, (a - high.astype(jnp.float32)).astype(jnp.bfloat16)


def permuted(a, turn):
    high, low = halves(a)
    turn = turn.astype(jnp.bfloat16)
    return product(high, turn, ((1,), (0,))) + product(low, turn, ((1,), (0,)))


def blurred(a, matrix, contract):
    high, low = halves(a)
    return product(high, matrix[0], contract) + (
        product(low, matrix[0], contract) + product(high, matrix[1], contract)
    )


def fused(tiles, data_ref, labels_ref, taps_ref, shift_ref, unpacked, raw, raw_labels, taps_buf, shift_buf, mixed, packed, packed_labels, held, held_labels, mats, est, coef, outgoing, incoming, leave, back, around, slab_coef, settled, sent, in_sem, data_sem, label_sem, mat_sem, swap_sem, back_sem, side_sem, send, send_side):
    mesh_id = pl.DeviceIdType.MESH
    slab, depth, rows = data_ref.shape[1:]
    lanes = packed.shape[2]
    fold = lanes // depth
    groups = rows // fold
    per_tile = groups // tiles
    width = held.shape[1]
    cells = held.shape[2]
    span = back.shape[1]
    pad = (span - slab) // 2
    view = lax.axis_index("view")
    tile = lax.axis_index("tile")
    part = lax.axis_index("parts")
    half = view // 2
    core = view % 2
    role = (half + tile) % 2
    flip_x = (view == 1) | (view == 2)
    flip_z = view >= 2

    def toggled(d):
        t = tile
        bit = 1
        while bit <= d:
            if d & bit:
                t = t + bit - 2 * bit * (t // bit % 2)
            bit *= 2
        return t

    others = [
        ((1 - half if away else half), toggled(d))
        for d in range(tiles - 1, -1, -1)
        for away in (1, 0)
        if d or away
    ]
    across = (part, 2 * half + 1 - core, tile)

    barrier = pltpu.get_barrier_semaphore()
    for h, t in others:
        pl.semaphore_signal(
            barrier, inc=1, device_id=(part, 2 * h + core, t), device_id_type=mesh_id
        )
    pl.semaphore_signal(barrier, inc=1, device_id=across, device_id_type=mesh_id)

    for source, target, sem in ((data_ref, raw, 0), (labels_ref, raw_labels, 1)):
        for x in range(slab):
            at = jnp.where(flip_x, slab - 1 - x, x)
            pltpu.make_async_copy(
                source.at[0, x],
                target.at[pl.ds(pl.multiple_of(at * depth, 8), depth)],
                in_sem.at[sem],
            ).start()
    small = [
        pltpu.make_async_copy(taps_ref, taps_buf, in_sem.at[2]),
        pltpu.make_async_copy(shift_ref, shift_buf, in_sem.at[3]),
    ]
    for copy in small:
        copy.start()

    def whole(ref, sem):
        pltpu.make_async_copy(ref, ref, sem).wait()

    same_block, turn = turning(lanes, depth, flip_z)
    slot = lax.broadcasted_iota(jnp.int32, (mixed.shape[1] // fold, lanes), 1) // depth
    blocks = slab * depth // lanes

    def pack(source, target, fill, turner):
        edge = jnp.full((1, slab, lanes), fill, jnp.float32)
        target[0:1] = edge
        target[groups + 1 : groups + 2] = edge
        for j in range(blocks):
            mixed[j, 0:rows] = turner(source[lanes * j : lanes * (j + 1), :])
        for j in range(blocks):
            parts = [
                mixed[j, pl.ds(b, mixed.shape[1] // fold, stride=fold), :] for b in range(fold)
            ]
            for k in range(fold):
                line = gathered(parts, [k] * fold, slot, depth)
                target[1 : groups + 1, fold * j + k, :] = line[:groups]

    def turned_labels(block):
        block = block.astype(jnp.float32).T.astype(jnp.bfloat16)
        return product(block, turn.astype(jnp.bfloat16), ((1,), (0,)))

    place = jnp.where(flip_x, tiles - 1 - tile, tile)
    spot = pl.ds(pl.multiple_of(place * slab, 8), slab)

    def scatter(source, target, sem):
        def piece(h, t):
            return source.at[pl.ds(per_tile * t + (h + t) % 2, width)]

        dst = target.at[half, :, spot, :]
        for h, t in others:
            pltpu.make_async_remote_copy(
                src_ref=piece(h, t),
                dst_ref=dst,
                send_sem=send,
                recv_sem=sem,
                device_id=(part, 2 * h + core, t),
                device_id_type=mesh_id,
            ).start()
        pltpu.make_async_copy(piece(half, tile), dst, sem).start()

    whole(raw, in_sem.at[0])
    pack(raw, packed, 1.0, lambda v: permuted(v.T, turn))
    pl.semaphore_wait(barrier, len(others) + 1)
    scatter(packed, held, data_sem)

    for copy in small:
        copy.wait()
    count = taps_buf.shape[0]
    taps = [jnp.concatenate([taps_buf[k]] * fold, axis=1) for k in range(count)]
    scale = taps[0]
    for k in range(1, count):
        scale = scale + taps[k]
    shift = jnp.concatenate([shift_buf[...]] * fold, axis=1)
    level = lax.broadcasted_iota(jnp.int32, (1, lanes), 1) % depth
    strip_row = lax.broadcasted_iota(jnp.int32, (depth, lanes), 0)
    strip_aim = jnp.where(flip_z, depth - 1 - strip_row, strip_row)
    strip = jnp.zeros((depth, lanes), jnp.float32)
    for k in range(count):
        index = jnp.clip(level + (k - 4) + shift, 0, depth - 1)
        strip = strip + jnp.where(index == strip_aim, taps[k] / scale, 0.0)
    strip = exact(strip, turn)
    mats[pl.ds(half, 1)] = strip[None]
    mat_copy = pltpu.make_async_remote_copy(
        src_ref=mats.at[half],
        dst_ref=mats.at[half],
        send_sem=send,
        recv_sem=mat_sem,
        device_id=(part, 2 * (1 - half) + core, tile),
        device_id_type=mesh_id,
    )
    mat_copy.start()

    whole(raw_labels, in_sem.at[1])
    pack(raw_labels, packed_labels, 0.0, turned_labels)
    scatter(packed_labels, held_labels, label_sem)

    inner_labels = packed_labels.at[pl.ds(1, groups)]

    def beside(side):
        onto = place + 1 - 2 * side
        t = jnp.where(flip_x, tiles - 1 - onto, onto)
        return pltpu.make_async_remote_copy(
            src_ref=inner_labels,
            dst_ref=around.at[:, pl.ds(2 * slab * side, slab), :],
            send_sem=send_side.at[side],
            recv_sem=side_sem.at[side],
            device_id=(part, view, jnp.clip(t, 0, tiles - 1)),
            device_id_type=mesh_id,
        )

    has_above = place < tiles - 1
    has_below = place > 0

    @pl.when(has_above)
    def _():
        beside(0).start()

    @pl.when(has_below)
    def _():
        beside(1).start()

    @pl.when(jnp.logical_not(has_below))
    def _():
        around[:, 0:slab, :] = jnp.zeros((groups, slab, lanes), jnp.float32)

    @pl.when(jnp.logical_not(has_above))
    def _():
        around[:, 2 * slab : 3 * slab, :] = jnp.zeros((groups, slab, lanes), jnp.float32)

    around[:, slab : 2 * slab, :] = packed_labels[1 : groups + 1]
    for s in range(2):
        for k in range(leave.shape[1]):
            leave[s, k, 0:pad] = jnp.zeros((pad, lanes), jnp.float32)
            leave[s, k, pad + cells : 2 * pad + cells] = jnp.zeros((pad, lanes), jnp.float32)

    lane = lax.broadcasted_iota(jnp.int32, (cells, lanes), 1)
    sub = lax.broadcasted_iota(jnp.int32, (cells, lanes), 0)
    first = per_tile * tile - 1 + role

    def lanes_of(field):
        return lane[: field.shape[0]]

    def ahead_y(fields, g):
        after = fields[(g + 1) % len(fields)]
        return jnp.where(
            lanes_of(fields[g]) < lanes - depth,
            pltpu.roll(fields[g], lanes - depth, 1),
            pltpu.roll(after, lanes - depth, 1),
        )

    def behind_y(fields, g):
        return jnp.where(
            lanes_of(fields[g]) < depth,
            pltpu.roll(fields[g - 1], depth, 1),
            pltpu.roll(fields[g], depth, 1),
        )

    def weights(regions, x_inside, y_first):
        strong, weak = TAU, TAU * WEAK
        high = regions[0].shape[0]
        count = len(regions)
        lane_of = lanes_of(regions[0])
        up_y = []
        for g in range(count):
            e_y = jnp.where(ahead_y(regions, g) == regions[g], strong, weak)
            y = fold * (y_first + g) + lane_of // depth
            up_y.append(jnp.where((y >= 0) & (y < rows - 1), e_y, 0.0))
        result = []
        for g in range(count):
            mine = regions[g]
            up_x = jnp.where(pltpu.roll(mine, high - 1, 0) == mine, strong, weak)
            up_x = jnp.where(x_inside, up_x, 0.0)
            up_z = jnp.where(pltpu.roll(mine, lanes - 1, 1) == mine, strong, weak)
            up_z = jnp.where(lane_of % depth == depth - 1, 0.0, up_z)
            down_x = pltpu.roll(up_x, 1, 0)
            down_z = pltpu.roll(up_z, 1, 1)
            down_y = behind_y(up_y, g)
            middle = 1.0 - (((up_x + down_x) + (up_z + down_z)) + (up_y[g] + down_y))
            result.append((middle, up_x, down_x, up_y[g], down_y, up_z, down_z))
        return result

    def swept(fields, factors, g):
        f = fields[g]
        high = f.shape[0]
        middle, up_x, down_x, up_y, down_y, up_z, down_z = factors
        return (
            (middle * f + up_x * pltpu.roll(f, high - 1, 0))
            + (down_x * pltpu.roll(f, 1, 0) + up_z * pltpu.roll(f, lanes - 1, 1))
        ) + (
            down_z * pltpu.roll(f, 1, 1)
            + (up_y * ahead_y(fields, g) + down_y * behind_y(fields, g))
        )

    def transposed(p, chosen):
        flipped = p.T
        result = []
        for g in chosen:
            piece = flipped[0:depth]
            if g:
                piece = pltpu.roll(piece, (lanes - depth * g) % lanes, 1)
            for b in range(1, fold):
                part_b = flipped[depth * b : depth * (b + 1)]
                amount = (depth * (b - g)) % lanes
                if amount:
                    part_b = pltpu.roll(part_b, amount, 1)
                piece = jnp.where(lane // depth == b, part_b, piece)
            result.append(piece)
        return result

    whole(held, data_sem)
    mat_copy.wait_recv()
    blurs = [
        halves(jnp.where(same_block, jnp.concatenate([mats[s]] * fold, axis=0), 0.0))
        for s in range(2)
    ]

    def paired_of(chosen, currents):
        corrections = []
        for s in range(2):
            recorded = jnp.concatenate([held[s, g] for g in chosen], axis=0)
            current = recorded if currents is None else jnp.concatenate(currents[s], axis=0)
            ratio = recorded / blurred(current, blurs[s], ((1,), (0,)))
            corrections.append(blurred(ratio, blurs[s], ((1,), (1,))))
        return jnp.sqrt(corrections[0] * corrections[1])

    def swapped_over(step, begin, size):
        copy = pltpu.make_async_remote_copy(
            src_ref=outgoing.at[step, pl.ds(begin, size)],
            dst_ref=incoming.at[step, pl.ds(begin, size)],
            send_sem=send,
            recv_sem=swap_sem.at[step],
            device_id=across,
            device_id_type=mesh_id,
        )
        copy.start()
        return copy

    paired = paired_of(range(width), None)
    for g, piece in enumerate(transposed(paired, range(width))):
        outgoing[0, g] = piece
    swap = swapped_over(0, 0, width)
    whole(held_labels, label_sem)
    for s in range(2):
        found = weights([held_labels[s, g] for g in range(width)], sub < cells - 1, first)
        for g in range(width):
            for i in range(len(found[g])):
                coef[i, s, g] = found[g][i]
    swap.wait_recv()
    joined = [
        jnp.sqrt(paired[cells * g : cells * (g + 1)] * incoming[0, g]) for g in range(width)
    ]
    fields = [[held[s, g] * joined[g] for g in range(width)] for s in range(2)]
    inner = range(1, width - 1)
    for sweep in range(SWEEPS):
        kept = inner if sweep == SWEEPS - 1 else range(width)
        fresh = [list(fields[s]) for s in range(2)]
        for s in range(2):
            for g in kept:
                factors = [coef[i, s, g] for i in range(coef.shape[0])]
                fresh[s][g] = swept(fields[s], factors, g)
        fields = fresh

    currents = [[fields[s][g] for g in inner] for s in range(2)]
    paired = paired_of(inner, currents)
    for s in range(2):
        for k in range(len(inner)):
            est[s, k] = currents[s][k]
    turned = transposed(jnp.concatenate([paired, paired], axis=0), range(len(inner)))
    for k, piece in enumerate(turned):
        outgoing[1, k] = piece
    swap = swapped_over(1, 0, len(inner))
    swap.wait_recv()
    for k in range(len(inner)):
        joined = jnp.sqrt(paired[cells * k : cells * (k + 1)] * incoming[1, k])
        for s in range(2):
            leave[s, k, pad : pad + cells] = est[s, k] * joined

    def window(h, t):
        flipped = core == 1 - h
        return pl.ds(pl.multiple_of(jnp.where(flipped, tiles - 1 - t, t) * slab, 8), span)

    own = pl.ds(per_tile * tile + role, len(inner))
    single = pl.ds(per_tile * tile + 2 * role, 1)
    for d in range(tiles - 1, -1, -1):
        t = toggled(d)
        pltpu.make_async_remote_copy(
            src_ref=leave.at[1 - half, pl.ds(role, 1), window(1 - half, t), :],
            dst_ref=back.at[single],
            send_sem=send,
            recv_sem=back_sem,
            device_id=(part, 2 * (1 - half) + core, t),
            device_id_type=mesh_id,
        ).start()
        mine = leave.at[half, :, window(half, t), :]
        if d == 0:
            pltpu.make_async_copy(mine, back.at[own], back_sem).start()
        else:
            pltpu.make_async_remote_copy(
                src_ref=mine,
                dst_ref=back.at[own],
                send_sem=send,
                recv_sem=back_sem,
                device_id=(part, 2 * half + core, t),
                device_id_type=mesh_id,
            ).start()

    @pl.when(has_below)
    def _():
        beside(0).wait_recv()

    @pl.when(has_above)
    def _():
        beside(1).wait_recv()

    x_at = place * slab - pad + sub[:span]
    x_inside = (x_at >= 0) & (x_at < cells - 1) & (sub[:span] < span - 1)
    found = weights([around[g, slab - pad : 2 * slab + pad] for g in range(groups)], x_inside, 0)
    for g in range(groups):
        for i in range(len(found[g])):
            slab_coef[i, g] = found[g][i]

    @pl.when(has_above)
    def _():
        beside(0).wait_send()

    @pl.when(has_below)
    def _():
        beside(1).wait_send()

    whole(sent, send)
    whole(back, back_sem)
    fields = [back[g] for g in range(groups)]
    for sweep in range(SWEEPS):
        fields = [
            swept(fields, [slab_coef[i, g] for i in range(slab_coef.shape[0])], g)
            for g in range(groups)
        ]
    for g in range(groups):
        settled[g] = fields[g][pad : pad + slab]
    for j in range(blocks):
        parts = []
        for k in range(fold):
            line = settled[:, fold * j + k, :]
            parts.append(
                jnp.concatenate(
                    [line, jnp.zeros((mixed.shape[1] // fold - groups, lanes), jnp.float32)], axis=0
                )
            )
        for b in range(fold):
            mixed[j, pl.ds(b, mixed.shape[1] // fold, stride=fold), :] = gathered(
                parts, [b] * fold, slot, depth
            )
        lined = permuted(mixed[j, 0:rows], turn).T
        for k in range(fold):
            x = fold * j + k
            at = jnp.where(flip_x, slab - 1 - x, x)
            unpacked[pl.ds(at, 1)] = lined[depth * k : depth * (k + 1)][None]


def by_rows(data, labels, kernel, offsets):
    tiles = lax.axis_size("tile")
    _, slab, rows, depth = data.shape
    fold = 128 // depth
    tall = -(-rows // (8 * fold)) * 8 * fold
    groups = rows // fold
    cells = slab * tiles
    width = 4
    kept = width - 2
    span = slab + 2 * SWEEPS
    flat = (slab * depth, rows)
    wide = (2, width, cells, 128)
    strips = (groups + 2, slab, 128)
    sent = (2 * (2 * tiles - 1) * width * slab + depth + (width + kept) * cells
            + ((tiles - 1) * kept + tiles) * span)
    dma = pltpu.SemaphoreType.DMA
    taps = kernel.transpose(2, 0, 1)
    ready = pl.pallas_call(
        functools.partial(fused, tiles),
        out_shape=pltpu.VMEM((slab, depth, rows), jnp.float32),
        in_specs=[pl.BlockSpec(memory_space=pltpu.HBM)] * 4,
        out_specs=pl.BlockSpec(memory_space=pltpu.VMEM),
        scratch_shapes=[
            pltpu.VMEM(flat, jnp.float32),
            pltpu.VMEM(flat, jnp.int32),
            pltpu.VMEM(taps.shape, jnp.float32),
            pltpu.VMEM(offsets.shape, jnp.int32),
            pltpu.VMEM((slab * depth // 128, tall, 128), jnp.float32),
            pltpu.VMEM(strips, jnp.float32),
            pltpu.VMEM(strips, jnp.float32),
            pltpu.VMEM(wide, jnp.float32),
            pltpu.VMEM(wide, jnp.float32),
            pltpu.VMEM((2, depth, 128), jnp.float32),
            pltpu.VMEM((2, kept, cells, 128), jnp.float32),
            pltpu.VMEM((7,) + wide, jnp.float32),
            pltpu.VMEM((ITERS,) + wide[1:], jnp.float32),
            pltpu.VMEM((ITERS,) + wide[1:], jnp.float32),
            pltpu.VMEM((2, kept, cells + span - slab, 128), jnp.float32),
            pltpu.VMEM((groups, span, 128), jnp.float32),
            pltpu.VMEM((groups, 3 * slab, 128), jnp.float32),
            pltpu.VMEM((7, groups, span, 128), jnp.float32),
            pltpu.VMEM((groups, slab, 128), jnp.float32),
            pltpu.VMEM((sent, 128), jnp.float32),
            dma((4,)),
            dma(()),
            dma(()),
            dma(()),
            dma((ITERS,)),
            dma(()),
            dma((2,)),
            dma(()),
            dma((2,)),
        ],
        compiler_params=pltpu.CompilerParams(
            collective_id=0, has_side_effects=True
        ),
    )(data.transpose(0, 1, 3, 2), labels.transpose(0, 1, 3, 2), taps, offsets)
    return ready[None].transpose(0, 1, 3, 2)


def fits(data, tiles, views):
    _, slab, rows, depth = data.shape
    return (
        views == 4
        and depth * 4 == 128
        and slab * tiles == depth
        and slab == 8
        and rows == 12 * tiles
    )


def program(data, labels, kernel, offsets):
    if fits(data, lax.axis_size("tile"), lax.axis_size("view")):
        return by_rows(data, labels, kernel, offsets)
    return on_device(data, labels, kernel, offsets)


def solution(mesh):
    placed = (
        P(("parts", "view"), "tile", None, None),
        P(("parts", "view"), "tile", None, None),
        P("view", None, None),
        P("view", None),
    )
    return jax.shard_map(
        program,
        mesh=mesh,
        in_specs=placed,
        out_specs=P(("parts", "view"), "tile", None, None),
        check_vma=False,
    )
```

time: 26.5 us -> 22 us (0.83)
  Pallas kernels: 26.2 us -> 21.1 us
  local copies, waits for them, and re-layouts: 0 us -> 0.66 us
    pallas_call x2 -> x1, Pallas kernels: 26.2 us -> 21.1 us  [by_rows(): pl.pallas_call(functools.partial(fused, tiles), out_shape=pltpu.VMEM((sla...]
    unnamed x0 -> x1, local copies, waits for them, and re-layouts: none -> 0.66 us
where the time goes in v1:
time: 22 us; the launch traced here: 21.8 us
  Pallas kernels  21.1 us (96%)
  local copies, waits for them, and re-layouts  0.66 us (3%)
    pallas_call x1, Pallas kernels, by_rows(): pl.pallas_call(functools.partial(fused, tiles), out_shape=pltpu.VMEM((sla...  21.1 us
    unnamed x1, local copies, waits for them, and re-layouts  0.66 us

profile of v1, /device:TPU:0, one launch (start us, length us, event | category | flops | bytes accessed | tf_op | source)
XLA Modules:
  0.0 21.8 jit_solution(9162068208043324570)
XLA Ops:
  0.0 21.1 %shard_map.46 = f32[8,32,48]{2,1,0:T(8,128)S(1)} custom-call(f32[1,8,32,48]{3,2,1,0:T(8,128)} %bitcast.7, s32[1,8,32,48]{3,2,1,0:T(8,128)} %bitcast.8, f32[9,1,32]{2,1,0:T(1,128)} %bitcast.9, s32[1,32]{1,0:T(1,128)} %shift_ref.1), custom_call_target="tpu_custom_call" | custom-call | tf_op jit(solution)/shard_map/pallas_call | solution.py:603
  21.1 0.7 %copy.6 = f32[1,8,48,32]{2,3,1,0:T(8,128)} copy(f32[1,8,48,32]{2,3,1,0:T(8,128)S(1)} %bitcast.6) | data formatting | bytes 98304

commit v2 on v1

--- a/solution.py
+++ b/solution.py
@@ -181,14 +181,14 @@
     )
 
 
-def fused(tiles, data_ref, labels_ref, taps_ref, shift_ref, unpacked, raw, raw_labels, taps_buf, shift_buf, mixed, packed, packed_labels, held, held_labels, mats, est, coef, outgoing, incoming, leave, back, around, slab_coef, settled, sent, in_sem, data_sem, label_sem, mat_sem, swap_sem, back_sem, side_sem, send, send_side):
+def fused(tiles, data_ref, labels_ref, taps_ref, shift_ref, unpacked, raw, raw_labels, taps_buf, shift_buf, mixed, packed, packed_labels, held, held_labels, mats, est, coef, outgoing, incoming, leave, back, around, slab_coef, settled, sent, in_sem, data_sem, label_sem, mat_sem, swap_sem, back_sem, side_sem, send, send_side, late_sem):
     mesh_id = pl.DeviceIdType.MESH
     slab, depth, rows = data_ref.shape[1:]
     lanes = packed.shape[2]
     fold = lanes // depth
     groups = rows // fold
-    per_tile = groups // tiles
     width = held.shape[1]
+    keep = width - 2
     cells = held.shape[2]
     span = back.shape[1]
     pad = (span - slab) // 2
@@ -197,32 +197,33 @@
     part = lax.axis_index("parts")
     half = view // 2
     core = view % 2
-    role = (half + tile) % 2
+    workers = tiles - 1
+    works = tile < workers
+    idle = tile >= workers
     flip_x = (view == 1) | (view == 2)
     flip_z = view >= 2
 
-    def toggled(d):
-        t = tile
-        bit = 1
-        while bit <= d:
-            if d & bit:
-                t = t + bit - 2 * bit * (t // bit % 2)
-            bit *= 2
-        return t
-
-    others = [
-        ((1 - half if away else half), toggled(d))
-        for d in range(tiles - 1, -1, -1)
-        for away in (1, 0)
-        if d or away
-    ]
+    def at_device(h, t):
+        return (part, 2 * h + core, t)
+
     across = (part, 2 * half + 1 - core, tile)
 
     barrier = pltpu.get_barrier_semaphore()
-    for h, t in others:
+
+    @pl.when(works)
+    def _():
+        for d in range(1, tiles):
+            for h in (1 - half, half):
+                pl.semaphore_signal(
+                    barrier,
+                    inc=1,
+                    device_id=at_device(h, (tile + d) % tiles),
+                    device_id_type=mesh_id,
+                )
         pl.semaphore_signal(
-            barrier, inc=1, device_id=(part, 2 * h + core, t), device_id_type=mesh_id
+            barrier, inc=1, device_id=at_device(1 - half, tile), device_id_type=mesh_id
         )
+
     pl.semaphore_signal(barrier, inc=1, device_id=across, device_id_type=mesh_id)
 
     for source, target, sem in ((data_ref, raw, 0), (labels_ref, raw_labels, 1)):
@@ -270,23 +271,46 @@
 
     def scatter(source, target, sem):
         def piece(h, t):
-            return source.at[pl.ds(per_tile * t + (h + t) % 2, width)]
+            return source.at[pl.ds(keep * (2 * t + h), width)]
 
         dst = target.at[half, :, spot, :]
-        for h, t in others:
+
+        def over(h, t):
             pltpu.make_async_remote_copy(
                 src_ref=piece(h, t),
                 dst_ref=dst,
                 send_sem=send,
                 recv_sem=sem,
-                device_id=(part, 2 * h + core, t),
+                device_id=at_device(h, t),
                 device_id_type=mesh_id,
             ).start()
-        pltpu.make_async_copy(piece(half, tile), dst, sem).start()
+
+        @pl.when(idle)
+        def _():
+            over(1 - half, 0)
+            over(half, 0)
+
+        for d in range(1, workers):
+            over(1 - half, (tile + d) % workers)
+            over(half, (tile + d) % workers)
+
+        @pl.when(works)
+        def _():
+            over(1 - half, tile)
+            pltpu.make_async_copy(piece(half, tile), dst, sem).start()
 
     whole(raw, in_sem.at[0])
     pack(raw, packed, 1.0, lambda v: permuted(v.T, turn))
-    pl.semaphore_wait(barrier, len(others) + 1)
+    pl.semaphore_wait(barrier, jnp.where(works, 2 * workers, 2 * workers + 1))
+
+    @pl.when(idle)
+    def _():
+        for d in range(workers):
+            for h in (1 - half, half):
+                pl.semaphore_signal(
+                    late_sem, inc=1, device_id=at_device(h, d), device_id_type=mesh_id
+                )
+
     scatter(packed, held, data_sem)
 
     for copy in small:
@@ -311,10 +335,10 @@
         dst_ref=mats.at[half],
         send_sem=send,
         recv_sem=mat_sem,
-        device_id=(part, 2 * (1 - half) + core, tile),
+        device_id=at_device(1 - half, tile),
         device_id_type=mesh_id,
     )
-    mat_copy.start()
+    pl.when(works)(mat_copy.start)
 
     whole(raw_labels, in_sem.at[1])
     pack(raw_labels, packed_labels, 0.0, turned_labels)
@@ -337,13 +361,14 @@
     has_above = place < tiles - 1
     has_below = place > 0
 
-    @pl.when(has_above)
-    def _():
-        beside(0).start()
-
-    @pl.when(has_below)
-    def _():
-        beside(1).start()
+    def start_sides():
+        @pl.when(has_above)
+        def _():
+            beside(0).start()
+
+        @pl.when(has_below)
+        def _():
+            beside(1).start()
 
     @pl.when(jnp.logical_not(has_below))
     def _():
@@ -361,7 +386,8 @@
 
     lane = lax.broadcasted_iota(jnp.int32, (cells, lanes), 1)
     sub = lax.broadcasted_iota(jnp.int32, (cells, lanes), 0)
-    first = per_tile * tile - 1 + role
+    block = 2 * tile + half
+    first = keep * block - 1
 
     def lanes_of(field):
         return lane[: field.shape[0]]
@@ -433,102 +459,107 @@
             result.append(piece)
         return result
 
-    whole(held, data_sem)
-    mat_copy.wait_recv()
-    blurs = [
-        halves(jnp.where(same_block, jnp.concatenate([mats[s]] * fold, axis=0), 0.0))
-        for s in range(2)
-    ]
-
-    def paired_of(chosen, currents):
-        corrections = []
+    @pl.when(works)
+    def _():
+        whole(held, data_sem)
+        mat_copy.wait_recv()
+        blurs = [
+            halves(jnp.where(same_block, jnp.concatenate([mats[s]] * fold, axis=0), 0.0))
+            for s in range(2)
+        ]
+
+        def paired_of(chosen, currents):
+            corrections = []
+            for s in range(2):
+                recorded = jnp.concatenate([held[s, g] for g in chosen], axis=0)
+                current = recorded if currents is None else jnp.concatenate(currents[s], axis=0)
+                ratio = recorded / blurred(current, blurs[s], ((1,), (0,)))
+                corrections.append(blurred(ratio, blurs[s], ((1,), (1,))))
+            return jnp.sqrt(corrections[0] * corrections[1])
+
+        def swapped_over(step, begin, size):
+            copy = pltpu.make_async_remote_copy(
+                src_ref=outgoing.at[step, pl.ds(begin, size)],
+                dst_ref=incoming.at[step, pl.ds(begin, size)],
+                send_sem=send,
+                recv_sem=swap_sem.at[step],
+                device_id=across,
+                device_id_type=mesh_id,
+            )
+            copy.start()
+            return copy
+
+        paired = paired_of(range(width), None)
+        for g, piece in enumerate(transposed(paired, range(width))):
+            outgoing[0, g] = piece
+        swap = swapped_over(0, 0, width)
+        pl.semaphore_wait(late_sem, 2)
+        start_sides()
+        whole(held_labels, label_sem)
         for s in range(2):
-            recorded = jnp.concatenate([held[s, g] for g in chosen], axis=0)
-            current = recorded if currents is None else jnp.concatenate(currents[s], axis=0)
-            ratio = recorded / blurred(current, blurs[s], ((1,), (0,)))
-            corrections.append(blurred(ratio, blurs[s], ((1,), (1,))))
-        return jnp.sqrt(corrections[0] * corrections[1])
-
-    def swapped_over(step, begin, size):
-        copy = pltpu.make_async_remote_copy(
-            src_ref=outgoing.at[step, pl.ds(begin, size)],
-            dst_ref=incoming.at[step, pl.ds(begin, size)],
-            send_sem=send,
-            recv_sem=swap_sem.at[step],
-            device_id=across,
-            device_id_type=mesh_id,
-        )
-        copy.start()
-        return copy
-
-    paired = paired_of(range(width), None)
-    for g, piece in enumerate(transposed(paired, range(width))):
-        outgoing[0, g] = piece
-    swap = swapped_over(0, 0, width)
-    whole(held_labels, label_sem)
-    for s in range(2):
-        found = weights([held_labels[s, g] for g in range(width)], sub < cells - 1, first)
-        for g in range(width):
-            for i in range(len(found[g])):
-                coef[i, s, g] = found[g][i]
-    swap.wait_recv()
-    joined = [
-        jnp.sqrt(paired[cells * g : cells * (g + 1)] * incoming[0, g]) for g in range(width)
-    ]
-    fields = [[held[s, g] * joined[g] for g in range(width)] for s in range(2)]
-    inner = range(1, width - 1)
-    for sweep in range(SWEEPS):
-        kept = inner if sweep == SWEEPS - 1 else range(width)
-        fresh = [list(fields[s]) for s in range(2)]
+            found = weights([held_labels[s, g] for g in range(width)], sub < cells - 1, first)
+            for g in range(width):
+                for i in range(len(found[g])):
+                    coef[i, s, g] = found[g][i]
+        swap.wait_recv()
+        joined = [
+            jnp.sqrt(paired[cells * g : cells * (g + 1)] * incoming[0, g]) for g in range(width)
+        ]
+        fields = [[held[s, g] * joined[g] for g in range(width)] for s in range(2)]
+        inner = range(1, width - 1)
+        for sweep in range(SWEEPS):
+            kept = inner if sweep == SWEEPS - 1 else range(width)
+            fresh = [list(fields[s]) for s in range(2)]
+            for s in range(2):
+                for g in kept:
+                    factors = [coef[i, s, g] for i in range(coef.shape[0])]
+                    fresh[s][g] = swept(fields[s], factors, g)
+            fields = fresh
+
+        currents = [[fields[s][g] for g in inner] for s in range(2)]
+        paired = paired_of(inner, currents)
         for s in range(2):
-            for g in kept:
-                factors = [coef[i, s, g] for i in range(coef.shape[0])]
-                fresh[s][g] = swept(fields[s], factors, g)
-        fields = fresh
-
-    currents = [[fields[s][g] for g in inner] for s in range(2)]
-    paired = paired_of(inner, currents)
-    for s in range(2):
+            for k in range(len(inner)):
+                est[s, k] = currents[s][k]
+        turned = transposed(jnp.concatenate([paired, paired], axis=0), range(len(inner)))
+        for k, piece in enumerate(turned):
+            outgoing[1, k] = piece
+        swap = swapped_over(1, 0, len(inner))
+        swap.wait_recv()
         for k in range(len(inner)):
-            est[s, k] = currents[s][k]
-    turned = transposed(jnp.concatenate([paired, paired], axis=0), range(len(inner)))
-    for k, piece in enumerate(turned):
-        outgoing[1, k] = piece
-    swap = swapped_over(1, 0, len(inner))
-    swap.wait_recv()
-    for k in range(len(inner)):
-        joined = jnp.sqrt(paired[cells * k : cells * (k + 1)] * incoming[1, k])
-        for s in range(2):
-            leave[s, k, pad : pad + cells] = est[s, k] * joined
-
-    def window(h, t):
-        flipped = core == 1 - h
-        return pl.ds(pl.multiple_of(jnp.where(flipped, tiles - 1 - t, t) * slab, 8), span)
-
-    own = pl.ds(per_tile * tile + role, len(inner))
-    single = pl.ds(per_tile * tile + 2 * role, 1)
-    for d in range(tiles - 1, -1, -1):
-        t = toggled(d)
-        pltpu.make_async_remote_copy(
-            src_ref=leave.at[1 - half, pl.ds(role, 1), window(1 - half, t), :],
-            dst_ref=back.at[single],
-            send_sem=send,
-            recv_sem=back_sem,
-            device_id=(part, 2 * (1 - half) + core, t),
-            device_id_type=mesh_id,
-        ).start()
-        mine = leave.at[half, :, window(half, t), :]
-        if d == 0:
-            pltpu.make_async_copy(mine, back.at[own], back_sem).start()
-        else:
-            pltpu.make_async_remote_copy(
-                src_ref=mine,
+            joined = jnp.sqrt(paired[cells * k : cells * (k + 1)] * incoming[1, k])
+            for s in range(2):
+                leave[s, k, pad : pad + cells] = est[s, k] * joined
+
+        def window(h, t):
+            flipped = core == 1 - h
+            return pl.ds(pl.multiple_of(jnp.where(flipped, tiles - 1 - t, t) * slab, 8), span)
+
+        def returned(h, t):
+            return pltpu.make_async_remote_copy(
+                src_ref=leave.at[h, :, window(h, t), :],
                 dst_ref=back.at[own],
                 send_sem=send,
                 recv_sem=back_sem,
-                device_id=(part, 2 * half + core, t),
+                device_id=at_device(h, t),
                 device_id_type=mesh_id,
-            ).start()
+            )
+
+        own = pl.ds(keep * block, keep)
+        for t in range(tiles):
+            returned(1 - half, t).start()
+
+            @pl.when(tile == t)
+            def _():
+                pltpu.make_async_copy(
+                    leave.at[half, :, window(half, t), :], back.at[own], back_sem
+                ).start()
+
+            @pl.when(tile != t)
+            def _():
+                returned(half, t).start()
+
+    pl.when(idle)(start_sides)
 
     @pl.when(has_below)
     def _():
@@ -553,7 +584,18 @@
     def _():
         beside(1).wait_send()
 
-    whole(sent, send)
+    share = width * slab
+    swaps = (width + keep) * cells
+    busy = 2 * (2 * workers - 1) * share + depth + swaps + (2 * tiles - 1) * keep * span
+
+    @pl.when(works)
+    def _():
+        whole(sent.at[pl.ds(0, busy)], send)
+
+    @pl.when(idle)
+    def _():
+        whole(sent.at[pl.ds(0, 4 * workers * share)], send)
+
     whole(back, back_sem)
     fields = [back[g] for g in range(groups)]
     for sweep in range(SWEEPS):
@@ -596,8 +638,7 @@
     flat = (slab * depth, rows)
     wide = (2, width, cells, 128)
     strips = (groups + 2, slab, 128)
-    sent = (2 * (2 * tiles - 1) * width * slab + depth + (width + kept) * cells
-            + ((tiles - 1) * kept + tiles) * span)
+    sent = 4 * tiles * width * slab + depth + (width + kept) * cells + 2 * tiles * kept * span
     dma = pltpu.SemaphoreType.DMA
     taps = kernel.transpose(2, 0, 1)
     ready = pl.pallas_call(
@@ -635,6 +676,7 @@
             dma((2,)),
             dma(()),
             dma((2,)),
+            pltpu.SemaphoreType.REGULAR,
         ],
         compiler_params=pltpu.CompilerParams(
             collective_id=0, has_side_effects=True
@@ -650,7 +692,8 @@
         and depth * 4 == 128
         and slab * tiles == depth
         and slab == 8
-        and rows == 12 * tiles
+        and tiles > 1
+        and rows == 16 * (tiles - 1)
     )
 
 

time: 22 us -> 19.8 us (0.900)
  Pallas kernels: 21.1 us -> 18.9 us
    pallas_call x1, Pallas kernels: 21.1 us -> 18.9 us  [by_rows(): pl.pallas_call(functools.partial(fused, tiles), out_shape=pltpu.VMEM((sla...]
where the time goes in v2:
time: 19.8 us; the launch traced here: 19.6 us
  Pallas kernels  18.9 us (95%)
  local copies, waits for them, and re-layouts  0.66 us (3%)
    pallas_call x1, Pallas kernels, by_rows(): pl.pallas_call(functools.partial(fused, tiles), out_shape=pltpu.VMEM((sla...  18.9 us
    unnamed x1, local copies, waits for them, and re-layouts  0.66 us

profile of v2, /device:TPU:0, one launch (start us, length us, event | category | flops | bytes accessed | tf_op | source)
XLA Modules:
  0.0 19.6 jit_solution(18442550251330040680)
XLA Ops:
  0.0 18.9 %shard_map.46 = f32[8,32,48]{2,1,0:T(8,128)S(1)} custom-call(f32[1,8,32,48]{3,2,1,0:T(8,128)} %bitcast.7, s32[1,8,32,48]{3,2,1,0:T(8,128)} %bitcast.8, f32[9,1,32]{2,1,0:T(1,128)} %bitcast.9, s32[1,32]{1,0:T(1,128)} %shift_ref.1), custom_call_target="tpu_custom_call" | custom-call | tf_op jit(solution)/shard_map/pallas_call | solution.py:644
  18.9 0.7 %copy.6 = f32[1,8,48,32]{2,3,1,0:T(8,128)} copy(f32[1,8,48,32]{2,3,1,0:T(8,128)S(1)} %bitcast.6) | data formatting | bytes 98304

commit v3 on v2

--- a/solution.py
+++ b/solution.py
@@ -197,9 +197,10 @@
     part = lax.axis_index("parts")
     half = view // 2
     core = view % 2
-    workers = tiles - 1
-    works = tile < workers
-    idle = tile >= workers
+    workers = tiles - 2
+    ends = tiles - workers
+    works = (tile > 0) & (tile <= workers)
+    idle = (tile == 0) | (tile > workers)
     flip_x = (view == 1) | (view == 2)
     flip_z = view >= 2
 
@@ -271,7 +272,7 @@
 
     def scatter(source, target, sem):
         def piece(h, t):
-            return source.at[pl.ds(keep * (2 * t + h), width)]
+            return source.at[pl.ds(keep * (2 * (t - 1) + h), width)]
 
         dst = target.at[half, :, spot, :]
 
@@ -287,15 +288,17 @@
 
         @pl.when(idle)
         def _():
-            over(1 - half, 0)
-            over(half, 0)
-
-        for d in range(1, workers):
-            over(1 - half, (tile + d) % workers)
-            over(half, (tile + d) % workers)
+            for d in range(workers):
+                t = jnp.where(tile == 0, workers - d, 1 + d)
+                over(1 - half, t)
+                over(half, t)
 
         @pl.when(works)
         def _():
+            for d in range(1, workers):
+                t = 1 + (tile - 1 + d) % workers
+                over(1 - half, t)
+                over(half, t)
             over(1 - half, tile)
             pltpu.make_async_copy(piece(half, tile), dst, sem).start()
 
@@ -305,10 +308,10 @@
 
     @pl.when(idle)
     def _():
-        for d in range(workers):
+        for t in range(1, workers + 1):
             for h in (1 - half, half):
                 pl.semaphore_signal(
-                    late_sem, inc=1, device_id=at_device(h, d), device_id_type=mesh_id
+                    late_sem, inc=1, device_id=at_device(h, t), device_id_type=mesh_id
                 )
 
     scatter(packed, held, data_sem)
@@ -342,6 +345,7 @@
 
     whole(raw_labels, in_sem.at[1])
     pack(raw_labels, packed_labels, 0.0, turned_labels)
+    pl.when((core == 1) & idle)(lambda: pl.delay(1200))
     scatter(packed_labels, held_labels, label_sem)
 
     inner_labels = packed_labels.at[pl.ds(1, groups)]
@@ -386,7 +390,7 @@
 
     lane = lax.broadcasted_iota(jnp.int32, (cells, lanes), 1)
     sub = lax.broadcasted_iota(jnp.int32, (cells, lanes), 0)
-    block = 2 * tile + half
+    block = 2 * (tile - 1) + half
     first = keep * block - 1
 
     def lanes_of(field):
@@ -443,20 +447,23 @@
             + (up_y * ahead_y(fields, g) + down_y * behind_y(fields, g))
         )
 
-    def transposed(p, chosen):
-        flipped = p.T
+    def transposed(p):
         result = []
-        for g in chosen:
-            piece = flipped[0:depth]
-            if g:
-                piece = pltpu.roll(piece, (lanes - depth * g) % lanes, 1)
-            for b in range(1, fold):
-                part_b = flipped[depth * b : depth * (b + 1)]
-                amount = (depth * (b - g)) % lanes
-                if amount:
-                    part_b = pltpu.roll(part_b, amount, 1)
-                piece = jnp.where(lane // depth == b, part_b, piece)
-            result.append(piece)
+        for start in range(0, p.shape[0] // cells, fold):
+            chunk = p[cells * start : cells * (start + fold)]
+            found = chunk.shape[0] // cells
+            flipped = jnp.concatenate([chunk] + [chunk[:cells]] * (fold - found), axis=0).T
+            for g in range(found):
+                piece = flipped[0:depth]
+                if g:
+                    piece = pltpu.roll(piece, (lanes - depth * g) % lanes, 1)
+                for b in range(1, fold):
+                    part_b = flipped[depth * b : depth * (b + 1)]
+                    amount = (depth * (b - g)) % lanes
+                    if amount:
+                        part_b = pltpu.roll(part_b, amount, 1)
+                    piece = jnp.where(lane // depth == b, part_b, piece)
+                result.append(piece)
         return result
 
     @pl.when(works)
@@ -490,10 +497,10 @@
             return copy
 
         paired = paired_of(range(width), None)
-        for g, piece in enumerate(transposed(paired, range(width))):
+        for g, piece in enumerate(transposed(paired)):
             outgoing[0, g] = piece
         swap = swapped_over(0, 0, width)
-        pl.semaphore_wait(late_sem, 2)
+        pl.semaphore_wait(late_sem, 2 * ends)
         start_sides()
         whole(held_labels, label_sem)
         for s in range(2):
@@ -521,8 +528,7 @@
         for s in range(2):
             for k in range(len(inner)):
                 est[s, k] = currents[s][k]
-        turned = transposed(jnp.concatenate([paired, paired], axis=0), range(len(inner)))
-        for k, piece in enumerate(turned):
+        for k, piece in enumerate(transposed(paired)):
             outgoing[1, k] = piece
         swap = swapped_over(1, 0, len(inner))
         swap.wait_recv()
@@ -546,7 +552,7 @@
             )
 
         own = pl.ds(keep * block, keep)
-        for t in range(tiles):
+        for t in [0, tiles - 1] + list(range(1, tiles - 1)):
             returned(1 - half, t).start()
 
             @pl.when(tile == t)
@@ -632,8 +638,8 @@
     tall = -(-rows // (8 * fold)) * 8 * fold
     groups = rows // fold
     cells = slab * tiles
-    width = 4
-    kept = width - 2
+    kept = groups // (2 * (tiles - 2))
+    width = kept + 2
     span = slab + 2 * SWEEPS
     flat = (slab * depth, rows)
     wide = (2, width, cells, 128)
@@ -692,8 +698,8 @@
         and depth * 4 == 128
         and slab * tiles == depth
         and slab == 8
-        and tiles > 1
-        and rows == 16 * (tiles - 1)
+        and tiles > 2
+        and rows % (8 * (tiles - 2)) == 0
     )
 
 

time: 19.8 us -> 19.4 us (0.980)
  Pallas kernels: 18.9 us -> 18.6 us
    pallas_call x1, Pallas kernels: 18.9 us -> 18.6 us  [by_rows(): pl.pallas_call(functools.partial(fused, tiles), out_shape=pltpu.VMEM((sla...]
where the time goes in v3:
time: 19.4 us; the launch traced here: 19.2 us
  Pallas kernels  18.6 us (96%)
  local copies, waits for them, and re-layouts  0.66 us (3%)
    pallas_call x1, Pallas kernels, by_rows(): pl.pallas_call(functools.partial(fused, tiles), out_shape=pltpu.VMEM((sla...  18.6 us
    unnamed x1, local copies, waits for them, and re-layouts  0.66 us

profile of v3, /device:TPU:0, one launch (start us, length us, event | category | flops | bytes accessed | tf_op | source)
XLA Modules:
  0.0 19.2 jit_solution(14402195651812216833)
XLA Ops:
  0.0 18.6 %shard_map.46 = f32[8,32,48]{2,1,0:T(8,128)S(1)} custom-call(f32[1,8,32,48]{3,2,1,0:T(8,128)} %bitcast.7, s32[1,8,32,48]{3,2,1,0:T(8,128)} %bitcast.8, f32[9,1,32]{2,1,0:T(1,128)} %bitcast.9, s32[1,32]{1,0:T(1,128)} %shift_ref.1), custom_call_target="tpu_custom_call" | custom-call | tf_op jit(solution)/shard_map/pallas_call | solution.py:650
  18.6 0.7 %copy.6 = f32[1,8,48,32]{2,3,1,0:T(8,128)} copy(f32[1,8,48,32]{2,3,1,0:T(8,128)S(1)} %bitcast.6) | data formatting | bytes 98304

commit v4 on v3

--- a/solution.py
+++ b/solution.py
@@ -174,11 +174,18 @@
     return product(high, turn, ((1,), (0,))) + product(low, turn, ((1,), (0,)))
 
 
-def blurred(a, matrix, contract):
-    high, low = halves(a)
-    return product(high, matrix[0], contract) + (
-        product(low, matrix[0], contract) + product(high, matrix[1], contract)
+def widened(matrix):
+    high, low = halves(matrix)
+    none = jnp.zeros_like(high)
+    return jnp.concatenate(
+        [jnp.concatenate([high, low], axis=1), jnp.concatenate([high, none], axis=1)], axis=0
     )
+
+
+def blurred(a, wide):
+    both = product(jnp.concatenate(halves(a), axis=1), wide, ((1,), (0,)))
+    lanes = a.shape[1]
+    return both[:, :lanes] + both[:, lanes:]
 
 
 def fused(tiles, data_ref, labels_ref, taps_ref, shift_ref, unpacked, raw, raw_labels, taps_buf, shift_buf, mixed, packed, packed_labels, held, held_labels, mats, est, coef, outgoing, incoming, leave, back, around, slab_coef, settled, sent, in_sem, data_sem, label_sem, mat_sem, swap_sem, back_sem, side_sem, send, send_side, late_sem):
@@ -345,7 +352,7 @@
 
     whole(raw_labels, in_sem.at[1])
     pack(raw_labels, packed_labels, 0.0, turned_labels)
-    pl.when((core == 1) & idle)(lambda: pl.delay(1200))
+    pl.when((core == 1) & idle)(lambda: pl.delay(2000))
     scatter(packed_labels, held_labels, label_sem)
 
     inner_labels = packed_labels.at[pl.ds(1, groups)]
@@ -468,20 +475,20 @@
 
     @pl.when(works)
     def _():
+        mat_copy.wait_recv()
+        blurs = []
+        for s in range(2):
+            matrix = jnp.where(same_block, jnp.concatenate([mats[s]] * fold, axis=0), 0.0)
+            blurs.append((widened(matrix), widened(matrix.T)))
         whole(held, data_sem)
-        mat_copy.wait_recv()
-        blurs = [
-            halves(jnp.where(same_block, jnp.concatenate([mats[s]] * fold, axis=0), 0.0))
-            for s in range(2)
-        ]
 
         def paired_of(chosen, currents):
             corrections = []
             for s in range(2):
                 recorded = jnp.concatenate([held[s, g] for g in chosen], axis=0)
                 current = recorded if currents is None else jnp.concatenate(currents[s], axis=0)
-                ratio = recorded / blurred(current, blurs[s], ((1,), (0,)))
-                corrections.append(blurred(ratio, blurs[s], ((1,), (1,))))
+                ratio = recorded / blurred(current, blurs[s][0])
+                corrections.append(blurred(ratio, blurs[s][1]))
             return jnp.sqrt(corrections[0] * corrections[1])
 
         def swapped_over(step, begin, size):
@@ -552,7 +559,10 @@
             )
 
         own = pl.ds(keep * block, keep)
-        for t in [0, tiles - 1] + list(range(1, tiles - 1)):
+        for t in (0, tiles - 1):
+            returned(0, t).start()
+            returned(1, t).start()
+        for t in range(1, tiles - 1):
             returned(1 - half, t).start()
 
             @pl.when(tile == t)

time: 19.4 us -> 18.5 us (0.954)
  Pallas kernels: 18.6 us -> 17.6 us
    pallas_call x1, Pallas kernels: 18.6 us -> 17.6 us  [by_rows(): pl.pallas_call(functools.partial(fused, tiles), out_shape=pltpu.VMEM((sla...]
where the time goes in v4:
time: 18.5 us; the launch traced here: 18.3 us
  Pallas kernels  17.6 us (95%)
  local copies, waits for them, and re-layouts  0.66 us (4%)
    pallas_call x1, Pallas kernels, by_rows(): pl.pallas_call(functools.partial(fused, tiles), out_shape=pltpu.VMEM((sla...  17.6 us
    unnamed x1, local copies, waits for them, and re-layouts  0.66 us

profile of v4, /device:TPU:0, one launch (start us, length us, event | category | flops | bytes accessed | tf_op | source)
XLA Modules:
  0.0 18.3 jit_solution(14596543782210828421)
XLA Ops:
  0.0 17.6 %shard_map.46 = f32[8,32,48]{2,1,0:T(8,128)S(1)} custom-call(f32[1,8,32,48]{3,2,1,0:T(8,128)} %bitcast.7, s32[1,8,32,48]{3,2,1,0:T(8,128)} %bitcast.8, f32[9,1,32]{2,1,0:T(1,128)} %bitcast.9, s32[1,32]{1,0:T(1,128)} %shift_ref.1), custom_call_target="tpu_custom_call" | custom-call | tf_op jit(solution)/shard_map/pallas_call | solution.py:660
  17.6 0.7 %copy.6 = f32[1,8,48,32]{2,3,1,0:T(8,128)} copy(f32[1,8,48,32]{2,3,1,0:T(8,128)S(1)} %bitcast.6) | data formatting | bytes 98304

commit v5 on v4

--- a/solution.py
+++ b/solution.py
@@ -234,6 +234,13 @@
 
     pl.semaphore_signal(barrier, inc=1, device_id=across, device_id_type=mesh_id)
 
+    small = [
+        pltpu.make_async_copy(taps_ref, taps_buf, in_sem.at[2]),
+        pltpu.make_async_copy(shift_ref, shift_buf, in_sem.at[3]),
+    ]
+    for copy in small:
+        copy.start()
+
     for source, target, sem in ((data_ref, raw, 0), (labels_ref, raw_labels, 1)):
         for x in range(slab):
             at = jnp.where(flip_x, slab - 1 - x, x)
@@ -242,13 +249,6 @@
                 target.at[pl.ds(pl.multiple_of(at * depth, 8), depth)],
                 in_sem.at[sem],
             ).start()
-    small = [
-        pltpu.make_async_copy(taps_ref, taps_buf, in_sem.at[2]),
-        pltpu.make_async_copy(shift_ref, shift_buf, in_sem.at[3]),
-    ]
-    for copy in small:
-        copy.start()
-
     def whole(ref, sem):
         pltpu.make_async_copy(ref, ref, sem).wait()
 
@@ -277,69 +277,54 @@
     place = jnp.where(flip_x, tiles - 1 - tile, tile)
     spot = pl.ds(pl.multiple_of(place * slab, 8), slab)
 
+    last = 2 * workers - 1
+    homes = [(h, t) for t in range(1, workers + 1) for h in range(2)]
+
     def scatter(source, target, sem):
-        def piece(h, t):
-            return source.at[pl.ds(keep * (2 * (t - 1) + h), width)]
-
-        dst = target.at[half, :, spot, :]
-
-        def over(h, t):
-            pltpu.make_async_remote_copy(
-                src_ref=piece(h, t),
-                dst_ref=dst,
-                send_sem=send,
-                recv_sem=sem,
-                device_id=at_device(h, t),
-                device_id_type=mesh_id,
-            ).start()
-
-        @pl.when(idle)
-        def _():
-            for d in range(workers):
-                t = jnp.where(tile == 0, workers - d, 1 + d)
-                over(1 - half, t)
-                over(half, t)
-
-        @pl.when(works)
-        def _():
-            for d in range(1, workers):
-                t = 1 + (tile - 1 + d) % workers
-                over(1 - half, t)
-                over(half, t)
-            over(1 - half, tile)
-            pltpu.make_async_copy(piece(half, tile), dst, sem).start()
-
-    whole(raw, in_sem.at[0])
-    pack(raw, packed, 1.0, lambda v: permuted(v.T, turn))
-    pl.semaphore_wait(barrier, jnp.where(works, 2 * workers, 2 * workers + 1))
-
-    @pl.when(idle)
-    def _():
-        for t in range(1, workers + 1):
-            for h in (1 - half, half):
-                pl.semaphore_signal(
-                    late_sem, inc=1, device_id=at_device(h, t), device_id_type=mesh_id
-                )
-
-    scatter(packed, held, data_sem)
+        for a in range(2):
+            for own in range(tiles):
+
+                @pl.when((half == a) & (tile == own))
+                def _():
+                    for h, t in sorted(homes, key=lambda ht: (-abs(ht[1] - own), ht[0] == a)):
+                        number = 2 * (t - 1) + h
+                        low = 1 if number == 0 else 0
+                        size = width - (number in (0, last))
+                        src = source.at[pl.ds(keep * number + low, size)]
+                        dst = target.at[a, pl.ds(low, size), spot, :]
+                        if (h, t) == (a, own):
+                            copy = pltpu.make_async_copy(src, dst, sem)
+                        else:
+                            copy = pltpu.make_async_remote_copy(
+                                src_ref=src,
+                                dst_ref=dst,
+                                send_sem=send,
+                                recv_sem=sem,
+                                device_id=at_device(h, t),
+                                device_id_type=mesh_id,
+                            )
+                        copy.start()
 
     for copy in small:
         copy.wait()
-    count = taps_buf.shape[0]
-    taps = [jnp.concatenate([taps_buf[k]] * fold, axis=1) for k in range(count)]
-    scale = taps[0]
-    for k in range(1, count):
-        scale = scale + taps[k]
-    shift = jnp.concatenate([shift_buf[...]] * fold, axis=1)
-    level = lax.broadcasted_iota(jnp.int32, (1, lanes), 1) % depth
-    strip_row = lax.broadcasted_iota(jnp.int32, (depth, lanes), 0)
-    strip_aim = jnp.where(flip_z, depth - 1 - strip_row, strip_row)
-    strip = jnp.zeros((depth, lanes), jnp.float32)
-    for k in range(count):
-        index = jnp.clip(level + (k - 4) + shift, 0, depth - 1)
-        strip = strip + jnp.where(index == strip_aim, taps[k] / scale, 0.0)
-    strip = exact(strip, turn)
-    mats[pl.ds(half, 1)] = strip[None]
+    @pl.when(works)
+    def _():
+        count = taps_buf.shape[0]
+        taps = [jnp.concatenate([taps_buf[k]] * fold, axis=1) for k in range(count)]
+        scale = taps[0]
+        for k in range(1, count):
+            scale = scale + taps[k]
+        shift = jnp.concatenate([shift_buf[...]] * fold, axis=1)
+        level = lax.broadcasted_iota(jnp.int32, (1, lanes), 1) % depth
+        strip_row = lax.broadcasted_iota(jnp.int32, (depth, lanes), 0)
+        strip_aim = jnp.where(flip_z, depth - 1 - strip_row, strip_row)
+        strip = jnp.zeros((depth, lanes), jnp.float32)
+        for k in range(count):
+            index = jnp.clip(level + (k - 4) + shift, 0, depth - 1)
+            strip = strip + jnp.where(index == strip_aim, taps[k] / scale, 0.0)
+        strip = exact(strip, turn)
+        mats[pl.ds(half, 1)] = strip[None]
+
     mat_copy = pltpu.make_async_remote_copy(
         src_ref=mats.at[half],
         dst_ref=mats.at[half],
@@ -348,7 +333,21 @@
         device_id=at_device(1 - half, tile),
         device_id_type=mesh_id,
     )
+
+    whole(raw, in_sem.at[0])
+    pack(raw, packed, 1.0, lambda v: permuted(v.T, turn))
+    pl.semaphore_wait(barrier, jnp.where(works, 2 * workers, 2 * workers + 1))
+
+    @pl.when(idle)
+    def _():
+        for t in range(1, workers + 1):
+            for h in (1 - half, half):
+                pl.semaphore_signal(
+                    late_sem, inc=1, device_id=at_device(h, t), device_id_type=mesh_id
+                )
+
     pl.when(works)(mat_copy.start)
+    scatter(packed, held, data_sem)
 
     whole(raw_labels, in_sem.at[1])
     pack(raw_labels, packed_labels, 0.0, turned_labels)
@@ -398,6 +397,24 @@
     lane = lax.broadcasted_iota(jnp.int32, (cells, lanes), 1)
     sub = lax.broadcasted_iota(jnp.int32, (cells, lanes), 0)
     block = 2 * (tile - 1) + half
+    edge = (block == 0) | (block == last)
+
+    def landed(ref, fill, sem):
+        @pl.when(edge)
+        def _():
+            whole(ref.at[:, pl.ds(0, width - 1)], sem)
+
+        @pl.when(jnp.logical_not(edge))
+        def _():
+            whole(ref, sem)
+
+        for number, slot_at in ((0, 0), (last, width - 1)):
+
+            @pl.when(block == number)
+            def _():
+                for s in range(2):
+                    ref[s, slot_at] = jnp.full((cells, lanes), fill, jnp.float32)
+
     first = keep * block - 1
 
     def lanes_of(field):
@@ -418,23 +435,27 @@
             pltpu.roll(fields[g], depth, 1),
         )
 
-    def weights(regions, x_inside, y_first):
-        strong, weak = TAU, TAU * WEAK
+    def steps(mask):
+        return jnp.where(mask, TAU, 0.0), jnp.where(mask, TAU * WEAK, 0.0)
+
+    def limits(high, count, x_inside, y_first):
+        lane_of = lane[:high]
+        along_y = []
+        for g in range(count):
+            y = fold * (y_first + g) + lane_of // depth
+            along_y.append(steps((y >= 0) & (y < rows - 1)))
+        return steps(x_inside), along_y, steps(lane_of % depth < depth - 1)
+
+    def weights(regions, bounds):
+        along_x, along_y, along_z = bounds
         high = regions[0].shape[0]
         count = len(regions)
-        lane_of = lanes_of(regions[0])
-        up_y = []
-        for g in range(count):
-            e_y = jnp.where(ahead_y(regions, g) == regions[g], strong, weak)
-            y = fold * (y_first + g) + lane_of // depth
-            up_y.append(jnp.where((y >= 0) & (y < rows - 1), e_y, 0.0))
+        up_y = [jnp.where(ahead_y(regions, g) == regions[g], *along_y[g]) for g in range(count)]
         result = []
         for g in range(count):
             mine = regions[g]
-            up_x = jnp.where(pltpu.roll(mine, high - 1, 0) == mine, strong, weak)
-            up_x = jnp.where(x_inside, up_x, 0.0)
-            up_z = jnp.where(pltpu.roll(mine, lanes - 1, 1) == mine, strong, weak)
-            up_z = jnp.where(lane_of % depth == depth - 1, 0.0, up_z)
+            up_x = jnp.where(pltpu.roll(mine, high - 1, 0) == mine, *along_x)
+            up_z = jnp.where(pltpu.roll(mine, lanes - 1, 1) == mine, *along_z)
             down_x = pltpu.roll(up_x, 1, 0)
             down_z = pltpu.roll(up_z, 1, 1)
             down_y = behind_y(up_y, g)
@@ -476,11 +497,12 @@
     @pl.when(works)
     def _():
         mat_copy.wait_recv()
+        bounds = limits(cells, width, sub < cells - 1, first)
         blurs = []
         for s in range(2):
             matrix = jnp.where(same_block, jnp.concatenate([mats[s]] * fold, axis=0), 0.0)
             blurs.append((widened(matrix), widened(matrix.T)))
-        whole(held, data_sem)
+        landed(held, 1.0, data_sem)
 
         def paired_of(chosen, currents):
             corrections = []
@@ -509,9 +531,9 @@
         swap = swapped_over(0, 0, width)
         pl.semaphore_wait(late_sem, 2 * ends)
         start_sides()
-        whole(held_labels, label_sem)
+        landed(held_labels, 0.0, label_sem)
         for s in range(2):
-            found = weights([held_labels[s, g] for g in range(width)], sub < cells - 1, first)
+            found = weights([held_labels[s, g] for g in range(width)], bounds)
             for g in range(width):
                 for i in range(len(found[g])):
                     coef[i, s, g] = found[g][i]
@@ -559,9 +581,10 @@
             )
 
         own = pl.ds(keep * block, keep)
-        for t in (0, tiles - 1):
-            returned(0, t).start()
-            returned(1, t).start()
+        returned(0, 0).start()
+        returned(1, tiles - 1).start()
+        returned(0, tiles - 1).start()
+        returned(1, 0).start()
         for t in range(1, tiles - 1):
             returned(1 - half, t).start()
 
@@ -587,7 +610,8 @@
 
     x_at = place * slab - pad + sub[:span]
     x_inside = (x_at >= 0) & (x_at < cells - 1) & (sub[:span] < span - 1)
-    found = weights([around[g, slab - pad : 2 * slab + pad] for g in range(groups)], x_inside, 0)
+    bounds = limits(span, groups, x_inside, 0)
+    found = weights([around[g, slab - pad : 2 * slab + pad] for g in range(groups)], bounds)
     for g in range(groups):
         for i in range(len(found[g])):
             slab_coef[i, g] = found[g][i]
@@ -600,18 +624,17 @@
     def _():
         beside(1).wait_send()
 
-    share = width * slab
     swaps = (width + keep) * cells
-    busy = 2 * (2 * workers - 1) * share + depth + swaps + (2 * tiles - 1) * keep * span
-
-    @pl.when(works)
-    def _():
-        whole(sent.at[pl.ds(0, busy)], send)
-
-    @pl.when(idle)
-    def _():
-        whole(sent.at[pl.ds(0, 4 * workers * share)], send)
-
+    pieces = 2 * workers * width - 2
+
+    def all_sent(kept_back, more):
+        whole(sent.at[pl.ds(0, 2 * (pieces - kept_back) * slab + more)], send)
+
+    after = depth + swaps + (2 * tiles - 1) * keep * span
+    pl.when(works & edge)(lambda: all_sent(width - 1, after))
+    pl.when(works & jnp.logical_not(edge))(lambda: all_sent(width, after))
+    pl.when(idle)(lambda: all_sent(0, 0))
+    turned_twice = turn.astype(jnp.bfloat16)
     whole(back, back_sem)
     fields = [back[g] for g in range(groups)]
     for sweep in range(SWEEPS):
@@ -634,7 +657,11 @@
             mixed[j, pl.ds(b, mixed.shape[1] // fold, stride=fold), :] = gathered(
                 parts, [b] * fold, slot, depth
             )
-        lined = permuted(mixed[j, 0:rows], turn).T
+        lined = product(
+            jnp.concatenate([turned_twice] * 2, axis=1),
+            jnp.concatenate(halves(mixed[j, 0:rows]), axis=1),
+            ((1,), (1,)),
+        )
         for k in range(fold):
             x = fold * j + k
             at = jnp.where(flip_x, slab - 1 - x, x)

time: 18.5 us -> 18.3 us (0.989)
  no operation moved by 1% of the time
where the time goes in v5:
time: 18.3 us; the launch traced here: 18.2 us
  Pallas kernels  17.5 us (96%)
  local copies, waits for them, and re-layouts  0.66 us (4%)
    pallas_call x1, Pallas kernels, by_rows(): pl.pallas_call(functools.partial(fused, tiles), out_shape=pltpu.VMEM((sla...  17.5 us
    unnamed x1, local copies, waits for them, and re-layouts  0.66 us

profile of v5, /device:TPU:0, one launch (start us, length us, event | category | flops | bytes accessed | tf_op | source)
XLA Modules:
  0.0 18.2 jit_solution(12068478797840187595)
XLA Ops:
  0.0 17.5 %shard_map.46 = f32[8,32,48]{2,1,0:T(8,128)S(1)} custom-call(f32[1,8,32,48]{3,2,1,0:T(8,128)} %bitcast.7, s32[1,8,32,48]{3,2,1,0:T(8,128)} %bitcast.8, f32[9,1,32]{2,1,0:T(1,128)} %bitcast.9, s32[1,32]{1,0:T(1,128)} %shift_ref.1), custom_call_target="tpu_custom_call" | custom-call | tf_op jit(solution)/shard_map/pallas_call | solution.py:687
  17.5 0.7 %copy.6 = f32[1,8,48,32]{2,3,1,0:T(8,128)} copy(f32[1,8,48,32]{2,3,1,0:T(8,128)S(1)} %bitcast.6) | data formatting | bytes 98304

commit v6 on v5

--- a/solution.py
+++ b/solution.py
@@ -351,7 +351,7 @@
 
     whole(raw_labels, in_sem.at[1])
     pack(raw_labels, packed_labels, 0.0, turned_labels)
-    pl.when((core == 1) & idle)(lambda: pl.delay(2000))
+    pl.when((core == 1) & idle)(lambda: pl.delay(2200))
     scatter(packed_labels, held_labels, label_sem)
 
     inner_labels = packed_labels.at[pl.ds(1, groups)]
@@ -582,9 +582,9 @@
 
         own = pl.ds(keep * block, keep)
         returned(0, 0).start()
+        returned(1, 0).start()
         returned(1, tiles - 1).start()
         returned(0, tiles - 1).start()
-        returned(1, 0).start()
         for t in range(1, tiles - 1):
             returned(1 - half, t).start()
 

time: 18.3 us -> 18.2 us (level)
  Pallas kernels: 17.5 us -> 17.3 us
    pallas_call x1, Pallas kernels: 17.5 us -> 17.3 us  [by_rows(): pl.pallas_call(functools.partial(fused, tiles), out_shape=pltpu.VMEM((sla...]
where the time goes in v6:
time: 18.2 us; the launch traced here: 18 us
  Pallas kernels  17.3 us (95%)
  local copies, waits for them, and re-layouts  0.66 us (4%)
    pallas_call x1, Pallas kernels, by_rows(): pl.pallas_call(functools.partial(fused, tiles), out_shape=pltpu.VMEM((sla...  17.3 us
    unnamed x1, local copies, waits for them, and re-layouts  0.66 us

profile of v6, /device:TPU:0, one launch (start us, length us, event | category | flops | bytes accessed | tf_op | source)
XLA Modules:
  0.0 18.0 jit_solution(13168820122183126519)
XLA Ops:
  0.0 17.3 %shard_map.46 = f32[8,32,48]{2,1,0:T(8,128)S(1)} custom-call(f32[1,8,32,48]{3,2,1,0:T(8,128)} %bitcast.7, s32[1,8,32,48]{3,2,1,0:T(8,128)} %bitcast.8, f32[9,1,32]{2,1,0:T(1,128)} %bitcast.9, s32[1,32]{1,0:T(1,128)} %shift_ref.1), custom_call_target="tpu_custom_call" | custom-call | tf_op jit(solution)/shard_map/pallas_call | solution.py:687
  17.3 0.7 %copy.6 = f32[1,8,48,32]{2,3,1,0:T(8,128)} copy(f32[1,8,48,32]{2,3,1,0:T(8,128)S(1)} %bitcast.6) | data formatting | bytes 98304

commit v7 on v6

--- a/solution.py
+++ b/solution.py
@@ -188,7 +188,7 @@
     return both[:, :lanes] + both[:, lanes:]
 
 
-def fused(tiles, data_ref, labels_ref, taps_ref, shift_ref, unpacked, raw, raw_labels, taps_buf, shift_buf, mixed, packed, packed_labels, held, held_labels, mats, est, coef, outgoing, incoming, leave, back, around, slab_coef, settled, sent, in_sem, data_sem, label_sem, mat_sem, swap_sem, back_sem, side_sem, send, send_side, late_sem):
+def fused(tiles, data_ref, labels_ref, taps_ref, shift_ref, unpacked, raw, raw_labels, taps_buf, shift_buf, mixed, packed, packed_labels, held, held_labels, mats, est, coef, outgoing, incoming, leave, back, around, slab_coef, settled, sent, in_sem, data_sem, label_sem, mat_sem, swap_sem, back_sem, side_sem, send, late_sem):
     mesh_id = pl.DeviceIdType.MESH
     slab, depth, rows = data_ref.shape[1:]
     lanes = packed.shape[2]
@@ -362,7 +362,7 @@
         return pltpu.make_async_remote_copy(
             src_ref=inner_labels,
             dst_ref=around.at[:, pl.ds(2 * slab * side, slab), :],
-            send_sem=send_side.at[side],
+            send_sem=send,
             recv_sem=side_sem.at[side],
             device_id=(part, view, jnp.clip(t, 0, tiles - 1)),
             device_id_type=mesh_id,
@@ -616,24 +616,17 @@
         for i in range(len(found[g])):
             slab_coef[i, g] = found[g][i]
 
-    @pl.when(has_above)
-    def _():
-        beside(0).wait_send()
-
-    @pl.when(has_below)
-    def _():
-        beside(1).wait_send()
-
     swaps = (width + keep) * cells
     pieces = 2 * workers * width - 2
 
     def all_sent(kept_back, more):
         whole(sent.at[pl.ds(0, 2 * (pieces - kept_back) * slab + more)], send)
 
-    after = depth + swaps + (2 * tiles - 1) * keep * span
+    sides = groups * slab
+    after = depth + swaps + (2 * tiles - 1) * keep * span + 2 * sides
     pl.when(works & edge)(lambda: all_sent(width - 1, after))
     pl.when(works & jnp.logical_not(edge))(lambda: all_sent(width, after))
-    pl.when(idle)(lambda: all_sent(0, 0))
+    pl.when(idle)(lambda: all_sent(0, sides))
     turned_twice = turn.astype(jnp.bfloat16)
     whole(back, back_sem)
     fields = [back[g] for g in range(groups)]
@@ -718,7 +711,6 @@
             dma(()),
             dma((2,)),
             dma(()),
-            dma((2,)),
             pltpu.SemaphoreType.REGULAR,
         ],
         compiler_params=pltpu.CompilerParams(

time: 18.2 us -> 18.1 us (level)
  no operation moved by 1% of the time
where the time goes in v7:
time: 18.1 us; the launch traced here: 18 us
  Pallas kernels  17.3 us (96%)
  local copies, waits for them, and re-layouts  0.66 us (4%)
    pallas_call x1, Pallas kernels, by_rows(): pl.pallas_call(functools.partial(fused, tiles), out_shape=pltpu.VMEM((sla...  17.3 us
    unnamed x1, local copies, waits for them, and re-layouts  0.66 us

profile of v7, /device:TPU:0, one launch (start us, length us, event | category | flops | bytes accessed | tf_op | source)
XLA Modules:
  0.0 18.0 jit_solution(252284469317817500)
XLA Ops:
  0.0 17.3 %shard_map.46 = f32[8,32,48]{2,1,0:T(8,128)S(1)} custom-call(f32[1,8,32,48]{3,2,1,0:T(8,128)} %bitcast.7, s32[1,8,32,48]{3,2,1,0:T(8,128)} %bitcast.8, f32[9,1,32]{2,1,0:T(1,128)} %bitcast.9, s32[1,32]{1,0:T(1,128)} %shift_ref.1), custom_call_target="tpu_custom_call" | custom-call | tf_op jit(solution)/shard_map/pallas_call | solution.py:680
  17.3 0.7 %copy.6 = f32[1,8,48,32]{2,3,1,0:T(8,128)} copy(f32[1,8,48,32]{2,3,1,0:T(8,128)S(1)} %bitcast.6) | data formatting | bytes 98304

commit v8 on v7

--- a/solution.py
+++ b/solution.py
@@ -257,9 +257,6 @@
     blocks = slab * depth // lanes
 
     def pack(source, target, fill, turner):
-        edge = jnp.full((1, slab, lanes), fill, jnp.float32)
-        target[0:1] = edge
-        target[groups + 1 : groups + 2] = edge
         for j in range(blocks):
             mixed[j, 0:rows] = turner(source[lanes * j : lanes * (j + 1), :])
         for j in range(blocks):

time: 18.1 us -> 18.1 us (level)
  no operation moved by 1% of the time
where the time goes in v8:
time: 18.1 us; the launch traced here: 18 us
  Pallas kernels  17.3 us (96%)
  local copies, waits for them, and re-layouts  0.66 us (4%)
    pallas_call x1, Pallas kernels, by_rows(): pl.pallas_call(functools.partial(fused, tiles), out_shape=pltpu.VMEM((sla...  17.3 us
    unnamed x1, local copies, waits for them, and re-layouts  0.66 us

profile of v8, /device:TPU:0, one launch (start us, length us, event | category | flops | bytes accessed | tf_op | source)
XLA Modules:
  0.0 18.0 jit_solution(2702508119280934427)
XLA Ops:
  0.0 17.3 %shard_map.46 = f32[8,32,48]{2,1,0:T(8,128)S(1)} custom-call(f32[1,8,32,48]{3,2,1,0:T(8,128)} %bitcast.7, s32[1,8,32,48]{3,2,1,0:T(8,128)} %bitcast.8, f32[9,1,32]{2,1,0:T(1,128)} %bitcast.9, s32[1,32]{1,0:T(1,128)} %shift_ref.1), custom_call_target="tpu_custom_call" | custom-call | tf_op jit(solution)/shard_map/pallas_call | solution.py:677
  17.3 0.7 %copy.6 = f32[1,8,48,32]{2,3,1,0:T(8,128)} copy(f32[1,8,48,32]{2,3,1,0:T(8,128)S(1)} %bitcast.6) | data formatting | bytes 98304
